TPU v7x, 32 devices: a whole 2x2x4 slice. The times are simulated.
32 devices in a mesh: tm: 16 (over z, y, core), space: 2 (over x).
Axes of the slice: x: 2, y: 2, z: 4, core: 2. Of those that a mesh axis runs over, the one named last changes fastest.
Arguments:
- iterate: float32 [16, 4, 128, 64, 128], P('tm', None, 'space'), may hold values from -6 to 6
- right_side: float32 [16, 4, 128, 64, 128], P('tm', None, 'space'), may hold values from -6 to 6
- diffusivity: float32 [128, 64, 128], P('space'), may hold values from 0.5 to 2
- velocity: float32 [3], replicated, may hold values from -2 to 2
Outputs:
- next_iterate: float32 [16, 4, 128, 64, 128], P('tm', None, 'space')
All inputs are finite; a program needn't handle non-finite values.
Results may differ from a plain program's by a relative error of at most 0.0003.
Values sent between devices are 32-bit elements; how exact they have to be, the bound alone decides.
A program may use at most 192 MiB of HBM per device.

v0:
```python
import functools
import math

import jax
import jax.numpy as jnp
import numpy as np
from jax import lax
from jax.experimental import pallas as pl
from jax.experimental.pallas import tpu as pltpu
from jax.sharding import PartitionSpec as P

diffusion_number = 16.0
circulant_alpha = 0.1


def collocation_matrix():
    radau_nodes = [0.08858795951270394, 0.4094668644407347, 0.7876594617608471, 1.0]
    matrix = [[0.0] * 4 for row_index in range(4)]
    for column_index in range(4):
        coefficients = [1.0]
        for other_index in range(4):
            if other_index != column_index:
                scale_value = 1.0 / (radau_nodes[column_index] - radau_nodes[other_index])
                shifted = [0.0] + [value * scale_value for value in coefficients]
                lowered = [
                    -radau_nodes[other_index] * scale_value * value for value in coefficients
                ] + [0.0]
                coefficients = [
                    left_value + right_value for left_value, right_value in zip(shifted, lowered)
                ]
        for row_index in range(4):
            total = 0.0
            for power_index in range(len(coefficients)):
                total = total + coefficients[power_index] * radau_nodes[row_index] ** (
                    power_index + 1
                ) / (power_index + 1)
            matrix[row_index][column_index] = total
    return matrix


def solve_system(matrix, target):
    count = len(target)
    rows_list = [list(matrix[row_index]) + [target[row_index]] for row_index in range(count)]
    for column in range(count):
        best_row = column
        for candidate in range(column + 1, count):
            if abs(rows_list[candidate][column]) > abs(rows_list[best_row][column]):
                best_row = candidate
        saved_row = rows_list[column]
        rows_list[column] = rows_list[best_row]
        rows_list[best_row] = saved_row
        leader = rows_list[column][column]
        for other_row in range(count):
            if other_row != column:
                factor = rows_list[other_row][column] / leader
                rows_list[other_row] = [
                    left_value - factor * right_value
                    for left_value, right_value in zip(rows_list[other_row], rows_list[column])
                ]
    return [
        rows_list[row_index][count] / rows_list[row_index][row_index] for row_index in range(count)
    ]


def node_basis():
    matrix = collocation_matrix()
    helper = [[0.0] * 4 for row_index in range(4)]
    coefficients = [0.0, 0.0, 0.0, 0.0, 1.0]
    for order in range(1, 5):
        product = [
            [
                sum((matrix[row_index][inner] * helper[inner][column] for inner in range(4)))
                for column in range(4)
            ]
            for row_index in range(4)
        ]
        for row_index in range(4):
            product[row_index][row_index] = product[row_index][row_index] + coefficients[5 - order]
        helper = product
        trace_value = sum(
            (
                sum((matrix[row_index][inner] * helper[inner][row_index] for inner in range(4)))
                for row_index in range(4)
            )
        )
        coefficients[4 - order] = -trace_value / order
    roots_list = [(0.4 + 0.9j) ** power_index for power_index in range(4)]
    for sweep in range(400):
        for root_index in range(4):
            current = roots_list[root_index]
            numer = 0.0
            for power_index in range(4, -1, -1):
                numer = numer * current + coefficients[power_index]
            denom = 1.0
            for other_index in range(4):
                if other_index != root_index:
                    denom = denom * (current - roots_list[other_index])
            roots_list[root_index] = current - numer / denom
    vectors = [[0.0] * 4 for row_index in range(4)]
    for root_index in range(4):
        shifted = [
            [
                matrix[row_index][column] - (roots_list[root_index] if row_index == column else 0.0)
                for column in range(3)
            ]
            for row_index in range(3)
        ]
        target = [-matrix[row_index][3] for row_index in range(3)]
        parts = solve_system(shifted, target) + [1.0 + 0j]
        for row_index in range(4):
            vectors[row_index][root_index] = parts[row_index]
    inverse = [[0.0] * 4 for row_index in range(4)]
    for column in range(4):
        unit = [1.0 if row_index == column else 0.0 for row_index in range(4)]
        parts = solve_system(vectors, unit)
        for row_index in range(4):
            inverse[row_index][column] = parts[row_index]
    weights = [sum((inverse[row_index][column] for column in range(4))) for row_index in range(4)]
    return (roots_list, vectors, inverse, weights)


def split_constant(matrix):
    high = matrix.astype(jnp.bfloat16)
    low = (matrix - high.astype(np.float64)).astype(jnp.bfloat16)
    return high, low


def split(value):
    high = value.astype(jnp.bfloat16)
    low = (value - high.astype(jnp.float32)).astype(jnp.bfloat16)
    return high, low


def dot(left, right):
    return jnp.dot(left, right, preferred_element_type=jnp.float32)


def table_times(high, low, value):
    value_high, value_low = split(value)
    return dot(high, value_high) + dot(high, value_low) + dot(low, value_high)


def times_table(value, high, low):
    value_high, value_low = split(value)
    return dot(value_high, high) + dot(value_low, high) + dot(value_high, low)


def tripled(value):
    high = value.astype(jnp.bfloat16).astype(jnp.float32)
    return jnp.concatenate((high, value - high, high), axis=0).astype(jnp.bfloat16)


def tripled_constant(matrix):
    high, low = split_constant(matrix)
    return np.concatenate((high, high, low), axis=1)


def complex_block(matrix):
    return np.block([[matrix.real, -matrix.imag], [matrix.imag, matrix.real]])


def fourier(rows, columns, length, sign):
    phases = np.outer(rows, columns) % length
    return np.exp(sign * 2j * np.pi * phases / length)


class Plan:
    def __init__(self, slabs, steps, size_x, size_z, size_y):
        self.slabs, self.steps = slabs, steps
        self.size_x, self.size_z, self.size_y = size_x, size_z, size_y
        self.long = long = size_x // slabs
        self.planes = size_z // 2 + 1
        each = -(-self.planes // slabs)
        while (each * slabs) % 2:
            each += 1
        self.each = each
        self.padded = each * slabs
        self.rows = 4 * self.padded
        self.block = 8
        self.blocks = long // self.block
        self.own_x = size_x // steps
        self.sent = 2 * long + 16
        self.values, self.vectors, self.inverse, self.weights = node_basis()
        self.matrix = np.array(collocation_matrix())

    def symbol_tables(self, length):
        theta_x = 2.0 * np.pi * np.arange(length)[:, None] / length
        theta_y = 2.0 * np.pi * np.arange(self.size_y)[None, :] / self.size_y
        real = diffusion_number * (2.0 * np.cos(theta_x) + 2.0 * np.cos(theta_y) - 4.0)
        ones = np.ones_like(real)
        return np.stack((real, np.sin(theta_x) * ones, np.sin(theta_y) * ones)).astype(np.float32)

    def z_symbols(self):
        theta = 2.0 * np.pi * np.arange(self.padded) / self.size_z
        return np.stack((diffusion_number * (2.0 * np.cos(theta) - 2.0), np.sin(theta))).astype(
            np.float32
        )

    def z_forward(self):
        wave = fourier(np.arange(self.padded), np.arange(self.size_z), self.size_z, -1.0)
        wave[self.planes :] = 0.0
        full = np.einsum("mn,kz->mknz", np.array(self.inverse), wave)
        full = full.reshape(self.rows, 4 * self.size_z)
        return np.concatenate((full.real, full.imag), axis=0)

    def z_backward(self):
        wave = fourier(np.arange(self.size_z), np.arange(self.padded), self.size_z, 1.0)
        weight = np.full(self.padded, 2.0)
        weight[0] = 1.0
        weight[self.planes - 1] = 1.0
        weight[self.planes :] = 0.0
        wave = wave * weight / self.size_z
        full = np.einsum("nm,zk->nzmk", np.array(self.vectors), wave)
        full = full.reshape(4 * self.size_z, self.rows)
        return np.concatenate((full.real, -full.imag), axis=1)

    def y_forward(self):
        span = np.arange(self.size_y)
        return complex_block(fourier(span, span, self.size_y, -1.0)).T

    def y_backward(self):
        span = np.arange(self.size_y)
        return complex_block(fourier(span, span, self.size_y, 1.0)).T / self.size_y

    def x_forward(self, length):
        span = np.arange(length)
        return complex_block(fourier(span, span, length, -1.0))

    def x_backward(self, length):
        span = np.arange(length)
        return complex_block(fourier(span, span, length, 1.0)) / length

    def ends(self):
        points = np.array([0, self.long - 1])
        wave = fourier(points, np.arange(self.long), self.long, 1.0) / self.long
        full = complex_block(wave)[[0, 2, 1, 3]]
        return np.concatenate((full, full, full, full), axis=0)

    def jump_sources(self):
        wave = np.arange(self.size_x)
        even = []
        for slab in range(self.slabs):
            start = slab * self.long

            def phase(point):
                return fourier(wave, np.array([point % self.size_x]), self.size_x, -1.0)[:, 0]

            first = phase(start - 1) - phase(start + self.long - 1)
            last = phase(start + self.long) - phase(start)
            even.append(np.stack((first, 1j * first, last, 1j * last), axis=1))
        return self.by_parity(even)

    def by_parity(self, blocks):
        zero = np.zeros_like(blocks[0])
        even = np.concatenate([part for block in blocks for part in (block, zero)], axis=1)
        odd = np.concatenate([part for block in blocks for part in (zero, block)], axis=1)
        return [np.concatenate((full.real, full.imag), axis=0) for full in (even, odd)]

    def end_sources(self):
        wave = np.arange(self.long)
        upper = fourier(wave, np.array([1]), self.long, 1.0)[:, 0]
        lower = np.ones_like(upper)
        return self.by_parity([np.stack((upper, 1j * upper, lower, 1j * lower), axis=1)])

    def jumps(self):
        wave = np.arange(self.size_x)
        rows = []
        for slab in range(self.slabs):
            start = slab * self.long
            points = np.array([start + self.long, start, start - 1, start + self.long - 1])
            value = fourier(points % self.size_x, wave, self.size_x, 1.0) / self.size_x
            upper, lower = value[0] - value[1], value[2] - value[3]
            full = complex_block(np.stack((upper, lower)))[[0, 2, 1, 3]]
            rows += [full, full]
        return np.concatenate(rows, axis=0)


def damped_by(real, imag, value):
    lower_real = 1.0 - (real * value.real - imag * value.imag)
    lower_imag = real * value.imag + imag * value.real
    scale = 1.0 / (lower_real * lower_real + lower_imag * lower_imag)
    return lower_real * scale, lower_imag * scale


def symbol(table, floats, wave_z, plane):
    real = table[0] + wave_z[0, plane]
    imag = -(floats[0] * table[1] + floats[1] * table[2] + floats[2] * wave_z[1, plane])
    return real, imag


def times(left, right):
    return (left[0] * right[0] - left[1] * right[1], left[0] * right[1] + left[1] * right[0])


def plus(left, right):
    return (left[0] + right[0], left[1] + right[1])


def number(value):
    value = complex(value)
    return (value.real, value.imag)


def end_scale(floats, shape):
    row = lax.broadcasted_iota(jnp.int32, shape, 0) % 4
    upper = diffusion_number - 0.5 * floats[0]
    lower = diffusion_number + 0.5 * floats[0]
    return jnp.where(row < 2, upper, lower)


def enter_kernel(plan, floats, it, below, above, low_halo, high_halo, right, diff, *refs):
    z_high, z_low, y_high, y_low, out_real, out_imag, buffer = refs
    block, rows, size_y = plan.block, plan.rows, plan.size_y
    at = pl.program_id(0)
    first, last = at == 0, at == pl.num_programs(0) - 1
    buffer[:, 1 : block + 1] = it[...]
    buffer[:, 0:1] = jnp.where(first, low_halo[...], below[...])
    buffer[:, block + 1 :] = jnp.where(last, high_halo[...], above[...])
    nodes = plan.matrix.sum(axis=1)
    size_z = plan.size_z

    def driving(plane):
        factor = diffusion_number * (diff[plane] - 1.0)
        terms = []
        for node in range(4):
            center = buffer[node, plane + 1]
            upper, lower = buffer[node, plane + 2], buffer[node, plane]
            z_up, z_down = pltpu.roll(center, size_z - 1, 0), pltpu.roll(center, 1, 0)
            y_up, y_down = pltpu.roll(center, size_y - 1, 1), pltpu.roll(center, 1, 1)
            laplace = (upper + lower) + (z_up + z_down) + (y_up + y_down) - 6.0 * center
            terms.append(factor * laplace)
        transport = (
            floats[0] * (upper - lower) + floats[1] * (y_up - y_down) + floats[2] * (z_up - z_down)
        )
        operated = floats[3] * (diffusion_number * laplace - 0.5 * transport)
        kept = floats[3] * center
        result = []
        for row in range(4):
            total = right[row, plane] + (float(nodes[row]) * operated - kept)
            for column in range(4):
                total = total + float(plan.matrix[row, column]) * terms[column]
            result.append(total)
        return jnp.concatenate(result, axis=0)

    def pair(index, carry):
        plane = 2 * index
        both = jnp.concatenate((driving(plane), driving(plane + 1)), axis=1)
        along_z = table_times(z_high[...], z_low[...], both)
        real, imag = along_z[:rows], along_z[rows:]
        stacked = jnp.concatenate(
            (
                jnp.concatenate((real[:, :size_y], imag[:, :size_y]), axis=1),
                jnp.concatenate((real[:, size_y:], imag[:, size_y:]), axis=1),
            ),
            axis=0,
        )
        along_y = times_table(stacked, y_high[...], y_low[...])
        for offset in range(2):
            part = along_y[offset * rows : (offset + 1) * rows]
            where = pl.ds(plane + offset, rows, stride=block)
            out_real[0, where, :] = part[:, :size_y]
            out_imag[0, where, :] = part[:, size_y:]
        return carry

    lax.fori_loop(0, block // 2, pair, 0)


def modes_kernel(plan, floats, wave_z, in_real, in_imag, table, *refs):
    f_high, f_low, b_high, b_low, e_high, e_low, out_real, out_imag, sent = refs
    long, size_y = plan.long, plan.size_y
    plane = pl.program_id(0)
    real = [in_real[:, mode, 0].reshape(long, size_y) for mode in range(4)]
    imag = [in_imag[:, mode, 0].reshape(long, size_y) for mode in range(4)]
    value = jnp.concatenate(
        (jnp.concatenate(real, axis=1), jnp.concatenate(imag, axis=1)), axis=0
    )
    spectrum = table_times(f_high[...], f_low[...], value)
    a_real, a_imag = symbol(table, floats, wave_z, plane)
    total, inner = None, []
    for mode in range(4):
        lanes = slice(mode * size_y, (mode + 1) * size_y)
        part = (spectrum[:long, lanes], spectrum[long:, lanes])
        out_real[0, mode], out_imag[0, mode] = part
        part = times(damped_by(a_real, a_imag, complex(plan.values[mode])), part)
        total = part if total is None else plus(total, part)
        inner.append(jnp.concatenate(part, axis=0))
    last = table_times(b_high[...], b_low[...], jnp.concatenate(total, axis=0))
    sent[0, : 2 * long] = last
    ends = table_times(e_high[...], e_low[...], jnp.concatenate(inner, axis=1))[:8]
    upper = lax.broadcasted_iota(jnp.int32, (8, size_y), 0) < 4
    for pair in range(2):
        even = ends[:, 2 * pair * size_y : (2 * pair + 1) * size_y]
        odd = ends[:, (2 * pair + 1) * size_y : (2 * pair + 2) * size_y]
        start = 2 * long + 8 * pair
        sent[0, start : start + 8] = jnp.where(upper, even, odd)


def end_spectra(plan, floats, tiles, even, odd):
    size_x, size_y = plan.size_x, plan.size_y
    pairs = []
    for pair in range(2):
        rows = jnp.concatenate([tiles[slab][8 * pair : 8 * pair + 8] for slab in range(plan.slabs)])
        pairs.append(rows * end_scale(floats, rows.shape))
    value = tripled(jnp.concatenate(pairs, axis=1))
    found = [dot(even[...], value), dot(odd[...], value)]
    result = []
    for mode in range(4):
        lanes = slice((mode // 2) * size_y, (mode // 2 + 1) * size_y)
        part = found[mode % 2][:, lanes]
        result.append(times(number(plan.values[mode]), (part[:size_x], part[size_x:])))
    return result


def last_kernel(plan, floats, wave_z, places, arrived, table, f_high, f_low, even, odd, out):
    long, size_x = plan.long, plan.size_x
    plane = places[1] * plan.each + pl.program_id(0)
    slabs = range(plan.slabs)
    value = jnp.concatenate(
        [arrived[slab, 0, :long] for slab in slabs]
        + [arrived[slab, 0, long : 2 * long] for slab in slabs],
        axis=0,
    )
    found = table_times(f_high[...], f_low[...], value)
    total = (found[:size_x], found[size_x:])
    tiles = [arrived[slab, 0, 2 * long :] for slab in slabs]
    sources = end_spectra(plan, floats, tiles, even, odd)
    a_real, a_imag = symbol(table, floats, wave_z, plane)
    for mode in range(4):
        damped = damped_by(a_real, a_imag, complex(plan.values[mode]))
        total = plus(total, times(damped, sources[mode]))
    own = plan.own_x
    for step in range(plan.steps):
        rows = slice(step * own, (step + 1) * own)
        out[step, 0, :own] = total[0][rows]
        out[step, 0, own:] = total[1][rows]


def sweep_kernel(plan, floats, wave_z, places, arrived, table, out):
    own = plan.own_x
    plane = places[1] * plan.each + pl.program_id(0)
    rows = pl.ds(pl.multiple_of(places[0] * own, own), own)
    a_real, a_imag = symbol([table[index, rows] for index in range(3)], floats, wave_z, plane)
    growth = None
    for mode in range(4):
        damped = damped_by(a_real, a_imag, complex(plan.values[mode]))
        term = times(number(plan.weights[mode]), damped)
        growth = term if growth is None else plus(growth, term)
    fields = [(arrived[step, 0, :own], arrived[step, 0, own:]) for step in range(plan.steps)]
    total, power = fields[0], growth
    for step in range(1, plan.steps):
        total = plus(fields[step], times(growth, total))
        power = times(growth, power)
    lower = (1.0 - circulant_alpha * power[0], -circulant_alpha * power[1])
    scale = circulant_alpha / (lower[0] * lower[0] + lower[1] * lower[1])
    current = times(total, (lower[0] * scale, -lower[1] * scale))
    for step in range(plan.steps):
        out[step, 0, :own] = current[0]
        out[step, 0, own:] = current[1]
        current = plus(fields[step], times(growth, current))


def driven_kernel(plan, floats, wave_z, places, before, arrived, table, *refs):
    b_high, b_low, even, odd, j_high, j_low, out = refs
    long, size_x, size_y, own = plan.long, plan.size_x, plan.size_y, plan.own_x
    plane = places[1] * plan.each + pl.program_id(0)
    real = jnp.concatenate([before[step, 0, :own] for step in range(plan.steps)], axis=0)
    imag = jnp.concatenate([before[step, 0, own:] for step in range(plan.steps)], axis=0)
    found = table_times(b_high[...], b_low[...], jnp.concatenate((real, imag), axis=0))
    tiles = [arrived[slab, 0] for slab in range(plan.slabs)]
    sources = end_spectra(plan, floats, tiles, even, odd)
    a_real, a_imag = symbol(table, floats, wave_z, plane)
    driven = []
    for mode in range(4):
        damped = damped_by(a_real, a_imag, complex(plan.values[mode]))
        weighted = times(number(plan.weights[mode]), (real, imag))
        driven.append(jnp.concatenate(times(damped, plus(weighted, sources[mode])), axis=0))
    jumps = table_times(j_high[...], j_low[...], jnp.concatenate(driven, axis=1))
    row = lax.broadcasted_iota(jnp.int32, (8, size_y), 0)
    for slab in range(plan.slabs):
        out[slab, 0, :long] = found[slab * long : (slab + 1) * long]
        out[slab, 0, long : 2 * long] = found[size_x + slab * long : size_x + (slab + 1) * long]
        above, under = tiles[(slab + 1) % plan.slabs], tiles[(slab - 1) % plan.slabs]
        for pair in range(2):
            part = slice(8 * pair, 8 * pair + 8)
            here = slice(8 * slab, 8 * slab + 8)
            local = jnp.where(row % 4 < 2, above[part], under[part]) - tiles[slab][part]
            first = jumps[here, 2 * pair * size_y : (2 * pair + 1) * size_y]
            second = jumps[here, (2 * pair + 1) * size_y : (2 * pair + 2) * size_y]
            start = 2 * long + 8 * pair
            out[slab, 0, start : start + 8] = local + jnp.where(row < 4, first, second)


def return_kernel(plan, floats, wave_z, arrived, in_real, in_imag, table, *refs):
    f_high, f_low, even, odd, b_high, b_low, out_real, out_imag = refs
    long, size_y = plan.long, plan.size_y
    plane = pl.program_id(0)
    found = table_times(f_high[...], f_low[...], arrived[0, : 2 * long])
    before = (found[:long], found[long:])
    ends = jnp.concatenate((arrived[0, 2 * long : 2 * long + 8], arrived[0, 2 * long + 8 :]), axis=1)
    value = tripled(ends * end_scale(floats, ends.shape))
    sources = [dot(even[...], value), dot(odd[...], value)]
    a_real, a_imag = symbol(table, floats, wave_z, plane)
    driven = []
    for mode in range(4):
        lanes = slice((mode // 2) * size_y, (mode // 2 + 1) * size_y)
        source = sources[mode % 2][:, lanes]
        total = times(number(plan.values[mode]), (source[:long], source[long:]))
        total = plus(total, times(number(plan.weights[mode]), before))
        total = plus(total, (in_real[0, mode], in_imag[0, mode]))
        damped = damped_by(a_real, a_imag, complex(plan.values[mode]))
        driven.append(jnp.concatenate(times(damped, total), axis=0))
    back = table_times(b_high[...], b_low[...], jnp.concatenate(driven, axis=1))
    for mode in range(4):
        lanes = slice(mode * size_y, (mode + 1) * size_y)
        shape = (plan.blocks, plan.block, size_y)
        out_real[:, mode, 0] = back[:long, lanes].reshape(shape)
        out_imag[:, mode, 0] = back[long:, lanes].reshape(shape)


def leave_kernel(plan, floats, in_real, in_imag, kept, y_high, y_low, z_high, z_low, z_rest, out):
    block, rows, size_y, size_z = plan.block, plan.rows, plan.size_y, plan.size_z
    most = z_high.shape[1]

    def pair(index, carry):
        plane = 2 * index
        parts = []
        for offset in range(2):
            where = pl.ds(plane + offset, rows, stride=block)
            parts.append(jnp.concatenate((in_real[0, where, :], in_imag[0, where, :]), axis=1))
        along_y = times_table(jnp.concatenate(parts, axis=0), y_high[...], y_low[...])
        stacked = jnp.concatenate(
            (
                jnp.concatenate((along_y[:rows, :size_y], along_y[rows:, :size_y]), axis=1),
                jnp.concatenate((along_y[:rows, size_y:], along_y[rows:, size_y:]), axis=1),
            ),
            axis=0,
        )
        found = table_times(z_high[...], z_low[...], stacked[:most])
        if most < 2 * rows:
            found = found + dot(z_rest[...], tripled(stacked[most:]))
        for offset in range(2):
            add = floats[3] * kept[0, plane + offset]
            for node in range(4):
                part = found[node * size_z : (node + 1) * size_z]
                out[node, plane + offset] = part[:, offset * size_y : (offset + 1) * size_y] + add
        return carry

    lax.fori_loop(0, block // 2, pair, 0)


def whole(array):
    zeros = (0,) * array.ndim
    return pl.BlockSpec(array.shape, lambda *at: zeros)


scalars = pl.BlockSpec(memory_space=pltpu.SMEM)


def called(kernel, name, grid, in_specs, out_specs, out_shape, operands, flops=0, scratch=()):
    return pl.pallas_call(
        kernel,
        name=name,
        grid=grid,
        in_specs=in_specs,
        out_specs=out_specs,
        out_shape=out_shape,
        scratch_shapes=list(scratch),
        compiler_params=pltpu.CompilerParams(
            dimension_semantics=("arbitrary",) * len(grid), vmem_limit_bytes=56 * 1024 * 1024
        ),
    )(*operands)


def shaped(*shape):
    return jax.ShapeDtypeStruct(shape, jnp.float32)


def shards(iterate, right_side, diffusivity, velocity):
    steps = lax.axis_size("tm")
    slabs = lax.axis_size("space")
    step = lax.axis_index("tm")
    slab = lax.axis_index("space")
    nodes, long, size_z, size_y = iterate.shape[1:]
    plan = Plan(slabs, steps, long * slabs, size_z, size_y)
    size_x, padded, each = plan.size_x, plan.padded, plan.each
    rows, block, blocks, sent_rows, own = plan.rows, plan.block, plan.blocks, plan.sent, plan.own_x
    iterate, right_side = iterate[0], right_side[0]

    is_last = (step == steps - 1).astype(jnp.float32)
    floats = jnp.concatenate((velocity, is_last[None]))
    places = jnp.stack((step, slab)).astype(jnp.int32)
    wave_z = jnp.asarray(plan.z_symbols())

    forward = [(index, (index + 1) % slabs) for index in range(slabs)]
    backward = [(target, source) for source, target in forward]
    low_halo = lax.ppermute(iterate[:, -1:], "space", forward)
    high_halo = lax.ppermute(iterate[:, :1], "space", backward)

    z_tables = split_constant(plan.z_forward())
    y_tables = split_constant(plan.y_forward())
    tables = list(z_tables + y_tables)
    thick = pl.BlockSpec((4, block, size_z, size_y), lambda at: (0, at, 0, 0))
    thin = (4, 1, size_z, size_y)
    out_block = pl.BlockSpec((1, rows * block, size_y), lambda at: (at, 0, 0))
    real, imag = called(
        functools.partial(enter_kernel, plan),
        "enter",
        (blocks,),
        [
            scalars,
            thick,
            pl.BlockSpec(thin, lambda at: (0, jnp.maximum(at * block - 1, 0), 0, 0)),
            pl.BlockSpec(thin, lambda at: (0, jnp.minimum(at * block + block, long - 1), 0, 0)),
            whole(low_halo),
            whole(high_halo),
            thick,
            pl.BlockSpec((block, size_z, size_y), lambda at: (at, 0, 0)),
        ]
        + [whole(table) for table in tables],
        [out_block, out_block],
        [shaped(blocks, rows * block, size_y)] * 2,
        [floats, iterate, iterate, iterate, low_halo, high_halo, right_side, diffusivity] + tables,
        scratch=[pltpu.VMEM((4, block + 2, size_z, size_y), jnp.float32)],
    )

    by_plane = (blocks, 4, padded, block, size_y)
    plane_block = pl.BlockSpec((blocks, 4, 1, block, size_y), lambda at: (0, 0, at, 0, 0))
    mode_block = pl.BlockSpec((1, 4, long, size_y), lambda at: (at, 0, 0, 0))
    sent_block = pl.BlockSpec((1, sent_rows, size_y), lambda at: (at, 0, 0))
    local_table = plan.symbol_tables(long)
    x_forward = split_constant(plan.x_forward(long))
    x_backward = split_constant(plan.x_backward(long))
    tables = list((local_table,) + x_forward + x_backward + split_constant(plan.ends()))
    mode_real, mode_imag, sent = called(
        functools.partial(modes_kernel, plan),
        "modes",
        (padded,),
        [scalars, scalars, plane_block, plane_block] + [whole(table) for table in tables],
        [mode_block, mode_block, sent_block],
        [shaped(padded, 4, long, size_y)] * 2 + [shaped(padded, sent_rows, size_y)],
        [floats, wave_z, real.reshape(by_plane), imag.reshape(by_plane)] + tables,
    )

    arrived = lax.all_to_all(
        sent.reshape(slabs, each, sent_rows, size_y), "space", 0, 0, tiled=True
    )
    full_table = plan.symbol_tables(size_x)
    all_forward = split_constant(plan.x_forward(size_x))
    all_backward = split_constant(plan.x_backward(size_x))
    sources = tuple(tripled_constant(matrix) for matrix in plan.jump_sources())
    slab_block = pl.BlockSpec((slabs, 1, sent_rows, size_y), lambda at: (0, at, 0, 0))
    step_block = pl.BlockSpec((steps, 1, 2 * own, size_y), lambda at: (0, at, 0, 0))
    step_shape = shaped(steps, each, 2 * own, size_y)
    tables = list((full_table,) + all_forward + sources)
    last = called(
        functools.partial(last_kernel, plan),
        "last",
        (each,),
        [scalars, scalars, scalars, slab_block] + [whole(table) for table in tables],
        step_block,
        step_shape,
        [floats, wave_z, places, arrived] + tables,
    )

    gathered = lax.all_to_all(last, "tm", 0, 0, tiled=True)
    before = called(
        functools.partial(sweep_kernel, plan),
        "sweep",
        (each,),
        [scalars, scalars, scalars, step_block, whole(full_table)],
        step_block,
        step_shape,
        [floats, wave_z, places, gathered, full_table],
    )
    before = lax.all_to_all(before, "tm", 0, 0, tiled=True)

    end_block = pl.BlockSpec((slabs, 1, 16, size_y), lambda at: (0, at, 2 * long // 16, 0))
    tables = list((full_table,) + all_backward + sources + split_constant(plan.jumps()))
    back = called(
        functools.partial(driven_kernel, plan),
        "driven",
        (each,),
        [scalars, scalars, scalars, step_block, end_block] + [whole(table) for table in tables],
        slab_block,
        shaped(slabs, each, sent_rows, size_y),
        [floats, wave_z, places, before, arrived] + tables,
    )
    back = lax.all_to_all(back, "space", 0, 0, tiled=True).reshape(padded, sent_rows, size_y)

    ends = tuple(tripled_constant(matrix) for matrix in plan.end_sources())
    tables = list((local_table,) + x_forward + ends + x_backward)
    real, imag = called(
        functools.partial(return_kernel, plan),
        "return",
        (padded,),
        [scalars, scalars, sent_block, mode_block, mode_block] + [whole(table) for table in tables],
        [plane_block, plane_block],
        [shaped(*by_plane)] * 2,
        [floats, wave_z, back, mode_real, mode_imag] + tables,
    )

    z_backward = plan.z_backward()
    most = min(256, 2 * rows)
    z_tables = split_constant(z_backward[:, :most])
    rest = z_backward[:, most:] if most < 2 * rows else z_backward[:, :16]
    tables = list(split_constant(plan.y_backward()) + z_tables) + [tripled_constant(rest)]
    result = called(
        functools.partial(leave_kernel, plan),
        "leave",
        (blocks,),
        [
            scalars,
            out_block,
            out_block,
            pl.BlockSpec((1, block, size_z, size_y), lambda at: (3, at, 0, 0)),
        ]
        + [whole(table) for table in tables],
        thick,
        shaped(4, long, size_z, size_y),
        [
            floats,
            real.reshape(blocks, rows * block, size_y),
            imag.reshape(blocks, rows * block, size_y),
            iterate,
        ]
        + tables,
    )
    return result[None]


def solution(mesh):
    placed = (
        P("tm", None, "space", None, None),
        P("tm", None, "space", None, None),
        P("space", None, None),
        P(),
    )
    return jax.shard_map(
        shards,
        mesh=mesh,
        in_specs=placed,
        out_specs=P("tm", None, "space", None, None),
        check_vma=False,
    )
```

profile of v0, /device:TPU:0, one launch (start us, length us, event | category | flops | bytes accessed | tf_op | source)
XLA Modules:
  0.0 358.1 jit_solution(1227398631679883343)
XLA Ops:
  0.0 1.0 fusion
  1.0 3.0 collective-permute-start.1
  4.0 0.1 collective-permute-start
  4.1 1.3 pad_maximum_fusion.floats
  5.4 2.9 collective-permute-done.1.high_halo
  8.4 0.0 copy-start.1
  8.4 2.0 collective-permute-done.low_halo
  10.3 0.0 copy-start.2
  10.3 0.0 copy-done.1
  10.3 0.6 copy-done.2
  11.0 34.1 %enter.1 = (f32[8,1088,128]{2,1,0:T(8,128)}, f32[8,1088,128]{2,1,0:T(8,128)}) custom-call(f32[4]{0:T(128)} %pad_maximum_fusion.floats, f32[4,64,64,128]{3,2,1,0:T(8,128)} %bitcast.13, f32[4,64,64,128]{3,2,1,0:T(8,128)} %bitcast.14, f32[4,64,64,128]{3,2,1,0:T(8,128)} %bitcast.15, f32[4,1,64,128]{3,2,1,0:T(8,128)} %copy-done.2, f32[4,1,64,128]{3,2,1,0:T(8,128)} %copy-done.1, ...), custom_call_target="tpu_custom_call" | custom-call | tf_op jit(solution)/shard_map/enter/pallas_call | solution.py:560
  45.1 27.8 %modes.1 = (f32[34,4,64,128]{3,2,1,0:T(8,128)}, f32[34,4,64,128]{3,2,1,0:T(8,128)}, f32[34,144,128]{2,1,0:T(8,128)}) custom-call(f32[4]{0:T(128)} %pad_maximum_fusion.floats, f32[2,34]{1,0:T(2,128)} %constant.66.clone.wave_z, f32[8,4,34,8,128]{4,3,2,1,0:T(8,128)} %bitcast.21, f32[8,4,34,8,128]{4,3,2,1,0:T(8,128)} %bitcast.22, ...), custom_call_target="tpu_custom_call" | custom-call | tf_op jit(solution)/shard_map/modes/pallas_call | solution.py:560
  72.9 3.8 %all-to-all-start = ((f32[2,17,144,128]{3,2,1,0:T(8,128)}), f32[2,17,144,128]{3,2,1,0:T(8,128)S(1)}, u32[]{:S(2)}, u32[]{:S(2)}) async-start(f32[2,17,144,128]{3,2,1,0:T(8,128)} %bitcast.23), calls=%async_computation | async-start | bytes 5013504 | tf_op jit(solution)/shard_map/all_to_all | solution.py:644
  76.7 0.6 pad_add_fusion.places
  77.3 28.3 %all-to-all-done.arrived = f32[2,17,144,128]{3,2,1,0:T(8,128)S(1)} async-done(((f32[2,17,144,128]{3,2,1,0:T(8,128)}), f32[2,17,144,128]{3,2,1,0:T(8,128)S(1)}, u32[]{:S(2)}, u32[]{:S(2)}) %all-to-all-start) | async-done | bytes 2506784 | tf_op jit(solution)/shard_map/all_to_all | solution.py:644
  105.6 0.0 copy-start
  105.6 1.5 copy-done
  107.1 14.2 %last.1 = f32[16,17,16,128]{3,2,1,0:T(8,128)} custom-call(f32[4]{0:T(128)} %pad_maximum_fusion.floats, f32[2,34]{1,0:T(2,128)} %constant.66.clone.wave_z, s32[2]{0:T(128)} %pad_add_fusion.places, f32[2,17,144,128]{3,2,1,0:T(8,128)} %copy-done, f32[3,128,128]{2,1,0:T(8,128)} %constant.78.clone.table, bf16[256,256]{1,0:T(8,128)(2,1)} %constant.79.clone.f_high, ...), custom_call_target="tpu_custom_call" | custom-call | tf_op jit(solution)/shard_map/last/pallas_call | solution.py:560
  121.2 58.0 %all_to_all.20.arrived = f32[16,17,16,128]{3,2,1,0:T(8,128)} all-to-all(f32[16,17,16,128]{3,2,1,0:T(8,128)} %last.1), channel_id=1, replica_groups=mesh['tm'=16,'space'=2] {'tm'}, dimensions={0} | all-to-all | bytes 4456448 | tf_op jit(solution)/shard_map/all_to_all | solution.py:665
  179.2 11.1 %sweep.1 = f32[16,17,16,128]{3,2,1,0:T(8,128)} custom-call(f32[4]{0:T(128)} %pad_maximum_fusion.floats, f32[2,34]{1,0:T(2,128)} %constant.66.clone.wave_z, s32[2]{0:T(128)} %pad_add_fusion.places, f32[16,17,16,128]{3,2,1,0:T(8,128)} %all_to_all.20.arrived, f32[3,128,128]{2,1,0:T(8,128)} %constant.78.clone.table), custom_call_target="tpu_custom_call" | custom-call | tf_op jit(solution)/shard_map/sweep/pallas_call | solution.py:560
  190.3 56.4 %all_to_all.21.before = f32[16,17,16,128]{3,2,1,0:T(8,128)} all-to-all(f32[16,17,16,128]{3,2,1,0:T(8,128)} %sweep.1), channel_id=1, replica_groups=mesh['tm'=16,'space'=2] {'tm'}, dimensions={0} | all-to-all | bytes 4456448 | tf_op jit(solution)/shard_map/all_to_all | solution.py:675
  246.7 17.7 %driven.1 = f32[2,17,144,128]{3,2,1,0:T(8,128)} custom-call(f32[4]{0:T(128)} %pad_maximum_fusion.floats, f32[2,34]{1,0:T(2,128)} %constant.66.clone.wave_z, s32[2]{0:T(128)} %pad_add_fusion.places, f32[16,17,16,128]{3,2,1,0:T(8,128)} %all_to_all.21.before, f32[2,17,144,128]{3,2,1,0:T(8,128)} %copy-done, f32[3,128,128]{2,1,0:T(8,128)} %constant.78.clone.table, ...), custom_call_target="tpu_custom_call" | custom-call | tf_op jit(solution)/shard_map/driven/pallas_call | solution.py:560
  264.4 35.9 %all_to_all.22 = f32[2,17,144,128]{3,2,1,0:T(8,128)} all-to-all(f32[2,17,144,128]{3,2,1,0:T(8,128)} %driven.1), channel_id=1, replica_groups=mesh['tm'=16,'space'=2] {'space'}, dimensions={0} | all-to-all | bytes 5013504 | tf_op jit(solution)/shard_map/all_to_all | solution.py:688
  300.3 30.4 %return.1 = (f32[8,4,34,8,128]{4,3,2,1,0:T(8,128)}, f32[8,4,34,8,128]{4,3,2,1,0:T(8,128)}) custom-call(f32[4]{0:T(128)} %pad_maximum_fusion.floats, f32[2,34]{1,0:T(2,128)} %constant.66.clone.wave_z, f32[34,144,128]{2,1,0:T(8,128)} %bitcast.17, f32[34,4,64,128]{3,2,1,0:T(8,128)} %get-tuple-element.15.in_real, f32[34,4,64,128]{3,2,1,0:T(8,128)} %get-tuple-element.16.in_imag, ...), custom_call_target="tpu_custom_call" | custom-call | tf_op jit(solution)/shard_map/return/pallas_call | solution.py:560
  330.8 27.3 %leave.1 = f32[4,64,64,128]{3,2,1,0:T(8,128)} custom-call(f32[4]{0:T(128)} %pad_maximum_fusion.floats, f32[8,1088,128]{2,1,0:T(8,128)} %bitcast.19, f32[8,1088,128]{2,1,0:T(8,128)} %bitcast.20, f32[4,64,64,128]{3,2,1,0:T(8,128)} %bitcast.16, bf16[256,256]{1,0:T(8,128)(2,1)} %constant.89.clone.y_high, bf16[256,256]{1,0:T(8,128)(2,1)} %constant.90.clone.y_low, ...), custom_call_target="tpu_custom_call" | custom-call | tf_op jit(solution)/shard_map/leave/pallas_call | solution.py:560
Async XLA Ops:
  1.0 7.4 %collective-permute-start.1 = (f32[4,1,64,128]{3,2,1,0:T(8,128)S(1)}, f32[4,1,64,128]{3,2,1,0:T(8,128)S(1)}, u32[]{:S(2)}, u32[]{:S(2)}) collective-permute-start(f32[4,1,64,128]{3,2,1,0:T(8,128)S(1)} %get-tuple-element.19), channel_id=1, source_target_pairs={{1,0},{0,1},{3,2},{2,3},{5,4},{4,5},{7,6},{6,7},{9,8},{8,9},{11,10... | collective-permute-start | bytes 393224 | tf_op jit(solution)/shard_map/ppermute | solution.py:597
  4.0 6.3 %collective-permute-start = (f32[4,1,64,128]{3,2,1,0:T(8,128)S(1)}, f32[4,1,64,128]{3,2,1,0:T(8,128)S(1)}, u32[]{:S(2)}, u32[]{:S(2)}) collective-permute-start(f32[4,1,64,128]{3,2,1,0:T(8,128)S(1)} %get-tuple-element.20), channel_id=1, source_target_pairs={{0,1},{1,0},{2,3},{3,2},{4,5},{5,4},{6,7},{7,6},{8,9},{9,8},{10,11... | collective-permute-start | bytes 393224 | tf_op jit(solution)/shard_map/ppermute | solution.py:596
  8.4 2.0 copy-start.1
  10.3 0.6 copy-start.2
  72.9 32.7 %all-to-all-start = ((f32[2,17,144,128]{3,2,1,0:T(8,128)}), f32[2,17,144,128]{3,2,1,0:T(8,128)S(1)}, u32[]{:S(2)}, u32[]{:S(2)}) async-start(f32[2,17,144,128]{3,2,1,0:T(8,128)} %bitcast.23), calls=%async_computation | async-start | bytes 5013504 | tf_op jit(solution)/shard_map/all_to_all | solution.py:644
  105.6 1.5 copy-start
where the time goes:
time: 361 us; the launch traced here: 358 us
  Pallas kernels  163 us (45%)
  blocking collectives  150 us (42%)
  waiting for transfers between devices  33.2 us (9%)
  starting transfers between devices  6.94 us (2%)
    pallas_call x7, Pallas kernels, called(): pl.pallas_call(kernel, name=name, grid=grid, in_specs=in_specs, out_specs...  163 us
    all_to_all x1, blocking collectives, shards(): gathered = lax.all_to_all(last, 'tm', 0, 0, tiled=True)  58 us
    all_to_all x1, blocking collectives, shards(): before = lax.all_to_all(before, 'tm', 0, 0, tiled=True)  56.4 us
    all_to_all x1, blocking collectives, shards(): lax.all_to_all(back, 'space', 0, 0, tiled=True)  35.9 us
    all_to_all x1, waiting for transfers between devices, shards(): lax.all_to_all(sent.reshape(slabs, each, sent_rows, size_y), 'space', 0,...  28.3 us
  transfers between devices with their start and end apart: 3, of which 3 were waited for; matrix products, arithmetic and copies ran while one was open for 1% of the time, Pallas kernels for 0%

commit v1 on v0

--- a/solution.py
+++ b/solution.py
@@ -11,6 +11,7 @@
 
 diffusion_number = 16.0
 circulant_alpha = 0.1
+MESH = pl.DeviceIdType.MESH
 
 
 def collocation_matrix():
@@ -411,83 +412,221 @@
     return result
 
 
-def last_kernel(plan, floats, wave_z, places, arrived, table, f_high, f_low, even, odd, out):
-    long, size_x = plan.long, plan.size_x
-    plane = places[1] * plan.each + pl.program_id(0)
-    slabs = range(plan.slabs)
-    value = jnp.concatenate(
-        [arrived[slab, 0, :long] for slab in slabs]
-        + [arrived[slab, 0, long : 2 * long] for slab in slabs],
-        axis=0,
-    )
-    found = table_times(f_high[...], f_low[...], value)
-    total = (found[:size_x], found[size_x:])
-    tiles = [arrived[slab, 0, 2 * long :] for slab in slabs]
-    sources = end_spectra(plan, floats, tiles, even, odd)
-    a_real, a_imag = symbol(table, floats, wave_z, plane)
-    for mode in range(4):
-        damped = damped_by(a_real, a_imag, complex(plan.values[mode]))
-        total = plus(total, times(damped, sources[mode]))
-    own = plan.own_x
-    for step in range(plan.steps):
-        rows = slice(step * own, (step + 1) * own)
-        out[step, 0, :own] = total[0][rows]
-        out[step, 0, own:] = total[1][rows]
-
-
-def sweep_kernel(plan, floats, wave_z, places, arrived, table, out):
-    own = plan.own_x
-    plane = places[1] * plan.each + pl.program_id(0)
-    rows = pl.ds(pl.multiple_of(places[0] * own, own), own)
-    a_real, a_imag = symbol([table[index, rows] for index in range(3)], floats, wave_z, plane)
-    growth = None
-    for mode in range(4):
-        damped = damped_by(a_real, a_imag, complex(plan.values[mode]))
-        term = times(number(plan.weights[mode]), damped)
-        growth = term if growth is None else plus(growth, term)
-    fields = [(arrived[step, 0, :own], arrived[step, 0, own:]) for step in range(plan.steps)]
-    total, power = fields[0], growth
-    for step in range(1, plan.steps):
-        total = plus(fields[step], times(growth, total))
-        power = times(growth, power)
-    lower = (1.0 - circulant_alpha * power[0], -circulant_alpha * power[1])
-    scale = circulant_alpha / (lower[0] * lower[0] + lower[1] * lower[1])
-    current = times(total, (lower[0] * scale, -lower[1] * scale))
-    for step in range(plan.steps):
-        out[step, 0, :own] = current[0]
-        out[step, 0, own:] = current[1]
-        current = plus(fields[step], times(growth, current))
-
-
-def driven_kernel(plan, floats, wave_z, places, before, arrived, table, *refs):
-    b_high, b_low, even, odd, j_high, j_low, out = refs
+def spread(plan, floats, wave_z, *refs):
+    (sent, table, f_high, f_low, even, odd, b_high, b_low, j_high, j_low, out) = refs[:11]
+    (x_in, f_send, f_all, growth, c_send, c_all, s_send, s_all, d_send, d_all, x_out) = refs[11:22]
+    (x_sems, f_sems, c_sems, s_sems, d_sems, y_sems, own_in, own_out) = refs[22:]
+    slabs, steps, each = plan.slabs, plan.steps, plan.each
     long, size_x, size_y, own = plan.long, plan.size_x, plan.size_y, plan.own_x
-    plane = places[1] * plan.each + pl.program_id(0)
-    real = jnp.concatenate([before[step, 0, :own] for step in range(plan.steps)], axis=0)
-    imag = jnp.concatenate([before[step, 0, own:] for step in range(plan.steps)], axis=0)
-    found = table_times(b_high[...], b_low[...], jnp.concatenate((real, imag), axis=0))
-    tiles = [arrived[slab, 0] for slab in range(plan.slabs)]
-    sources = end_spectra(plan, floats, tiles, even, odd)
-    a_real, a_imag = symbol(table, floats, wave_z, plane)
-    driven = []
-    for mode in range(4):
-        damped = damped_by(a_real, a_imag, complex(plan.values[mode]))
-        weighted = times(number(plan.weights[mode]), (real, imag))
-        driven.append(jnp.concatenate(times(damped, plus(weighted, sources[mode])), axis=0))
-    jumps = table_times(j_high[...], j_low[...], jnp.concatenate(driven, axis=1))
-    row = lax.broadcasted_iota(jnp.int32, (8, size_y), 0)
-    for slab in range(plan.slabs):
-        out[slab, 0, :long] = found[slab * long : (slab + 1) * long]
-        out[slab, 0, long : 2 * long] = found[size_x + slab * long : size_x + (slab + 1) * long]
-        above, under = tiles[(slab + 1) % plan.slabs], tiles[(slab - 1) % plan.slabs]
-        for pair in range(2):
-            part = slice(8 * pair, 8 * pair + 8)
-            here = slice(8 * slab, 8 * slab + 8)
-            local = jnp.where(row % 4 < 2, above[part], under[part]) - tiles[slab][part]
-            first = jumps[here, 2 * pair * size_y : (2 * pair + 1) * size_y]
-            second = jumps[here, (2 * pair + 1) * size_y : (2 * pair + 2) * size_y]
-            start = 2 * long + 8 * pair
-            out[slab, 0, start : start + 8] = local + jnp.where(row < 4, first, second)
+    half, pairs = size_x // 2, steps // 2
+    step, slab = lax.axis_index("tm"), lax.axis_index("space")
+    parity, place = step % 2, step // 2
+    other = (step + 1 - 2 * parity, slab)
+
+    def peer(index):
+        return (2 * index + parity, slab)
+
+    def slab_peer(index):
+        return (step, index)
+
+    barrier = pltpu.get_barrier_semaphore()
+    neighbours = [other]
+    neighbours += [slab_peer((slab + shift) % slabs) for shift in range(1, slabs)]
+    neighbours += [peer((place + shift) % pairs) for shift in range(1, pairs)]
+    for device in neighbours:
+        pl.semaphore_signal(barrier, inc=1, device_id=device, device_id_type=MESH)
+    pl.semaphore_wait(barrier, len(neighbours))
+
+    def remote(source, target, sems, plane, device):
+        return pltpu.make_async_remote_copy(
+            src_ref=source,
+            dst_ref=target,
+            send_sem=sems.at[0, plane],
+            recv_sem=sems.at[1, plane],
+            device_id=device,
+            device_id_type=MESH,
+        )
+
+    def await_all(ref, sems, kind, plane):
+        pltpu.make_async_copy(ref, ref, sems.at[kind, plane]).wait()
+
+    mine = pltpu.make_async_copy(sent.at[pl.ds(slab * each, each)], x_in.at[slab], own_in)
+    mine.start()
+
+    def start_plane(plane, carry):
+        for shift in range(1, slabs):
+            target = (slab + shift) % slabs
+            remote(
+                sent.at[target * each + plane],
+                x_in.at[slab, plane],
+                x_sems,
+                plane,
+                slab_peer(target),
+            ).start()
+        return carry
+
+    lax.fori_loop(0, each, start_plane, 0)
+    mine.wait()
+
+    def symbols(plane, start, count):
+        rows = pl.ds(start, count)
+        tables = [table[index, rows] for index in range(3)]
+        return symbol(tables, floats, wave_z, slab * each + plane)
+
+    def grown(plane, start, count):
+        a_real, a_imag = symbols(plane, start, count)
+        total = None
+        for mode in range(4):
+            damped = damped_by(a_real, a_imag, complex(plan.values[mode]))
+            term = times(number(plan.weights[mode]), damped)
+            total = term if total is None else plus(total, term)
+        return total
+
+    def spectrum_stage(plane):
+        if slabs > 1:
+            await_all(x_in.at[pl.ds(0, slabs - 1), plane], x_sems, 1, plane)
+        arrived = [x_in[index, plane] for index in range(slabs)]
+        value = jnp.concatenate(
+            [part[:long] for part in arrived] + [part[long : 2 * long] for part in arrived], axis=0
+        )
+        found = table_times(f_high[...], f_low[...], value)
+        total = (found[:size_x], found[size_x:])
+        sources = end_spectra(plan, floats, [part[2 * long :] for part in arrived], even, odd)
+        a_real, a_imag = symbols(plane, 0, size_x)
+        for mode in range(4):
+            damped = damped_by(a_real, a_imag, complex(plan.values[mode]))
+            total = plus(total, times(damped, sources[mode]))
+        for index in range(2):
+            rows = slice(index * half, (index + 1) * half)
+            lower, upper = total[index][:half], total[index][half:]
+            f_send[plane, rows] = jnp.where(parity == 0, upper, lower)
+            f_all[plane, parity, rows] = jnp.where(parity == 0, lower, upper)
+        remote(f_send.at[plane], f_all.at[plane, parity], f_sems, plane, other).start()
+
+    def pair_stage(plane):
+        factor = grown(plane, pl.multiple_of(parity * half, half), half)
+        growth[plane, :half], growth[plane, half:] = factor
+        await_all(f_send.at[plane], f_sems, 1, plane)
+        early = (f_all[plane, 0, :half], f_all[plane, 0, half:])
+        later = (f_all[plane, 1, :half], f_all[plane, 1, half:])
+        total = plus(later, times(factor, early))
+        for index in range(pairs):
+            rows = slice(index * own, (index + 1) * own)
+            c_send[index, plane, :own] = total[0][rows]
+            c_send[index, plane, own:] = total[1][rows]
+        c_all[place, plane] = c_send[place, plane]
+        for shift in range(1, pairs):
+            target = (place + shift) % pairs
+            remote(
+                c_send.at[target, plane], c_all.at[place, plane], c_sems, plane, peer(target)
+            ).start()
+
+    def sweep_stage(plane):
+        factor = grown(plane, pl.multiple_of(parity * half + place * own, own), own)
+        factor = times(factor, factor)
+        if pairs > 1:
+            await_all(c_all.at[pl.ds(0, pairs - 1), plane], c_sems, 1, plane)
+        fields = [(c_all[index, plane, :own], c_all[index, plane, own:]) for index in range(pairs)]
+        total, power = fields[0], factor
+        for index in range(1, pairs):
+            total = plus(fields[index], times(factor, total))
+            power = times(factor, power)
+        lower = (1.0 - circulant_alpha * power[0], -circulant_alpha * power[1])
+        scale = circulant_alpha / (lower[0] * lower[0] + lower[1] * lower[1])
+        current = times(total, (lower[0] * scale, -lower[1] * scale))
+        for index in range(pairs):
+            s_send[index, plane, :own] = current[0]
+            s_send[index, plane, own:] = current[1]
+            current = plus(fields[index], times(factor, current))
+        s_all[place, plane] = s_send[place, plane]
+        for shift in range(1, pairs):
+            target = (place + shift) % pairs
+            remote(
+                s_send.at[target, plane], s_all.at[place, plane], s_sems, plane, peer(target)
+            ).start()
+
+    def start_stage(plane):
+        if pairs > 1:
+            await_all(s_all.at[pl.ds(0, pairs - 1), plane], s_sems, 1, plane)
+        early = tuple(
+            jnp.concatenate([s_all[index, plane, rows] for index in range(pairs)], axis=0)
+            for rows in (slice(0, own), slice(own, 2 * own))
+        )
+        field = (f_all[plane, 0, :half], f_all[plane, 0, half:])
+        later = plus(field, times((growth[plane, :half], growth[plane, half:]), early))
+        for index in range(2):
+            rows = slice(index * half, (index + 1) * half)
+            d_send[plane, rows] = jnp.where(parity == 0, later[index], early[index])
+            d_all[plane, parity, rows] = jnp.where(parity == 0, early[index], later[index])
+        remote(d_send.at[plane], d_all.at[plane, parity], d_sems, plane, other).start()
+
+    def return_stage(plane):
+        await_all(d_send.at[plane], d_sems, 1, plane)
+        real = jnp.concatenate((d_all[plane, 0, :half], d_all[plane, 1, :half]), axis=0)
+        imag = jnp.concatenate((d_all[plane, 0, half:], d_all[plane, 1, half:]), axis=0)
+        found = table_times(b_high[...], b_low[...], jnp.concatenate((real, imag), axis=0))
+        tiles = [x_in[index, plane, 2 * long :] for index in range(slabs)]
+        sources = end_spectra(plan, floats, tiles, even, odd)
+        a_real, a_imag = symbols(plane, 0, size_x)
+        driven = []
+        for mode in range(4):
+            damped = damped_by(a_real, a_imag, complex(plan.values[mode]))
+            weighted = times(number(plan.weights[mode]), (real, imag))
+            driven.append(jnp.concatenate(times(damped, plus(weighted, sources[mode])), axis=0))
+        jumps = table_times(j_high[...], j_low[...], jnp.concatenate(driven, axis=1))
+        row = lax.broadcasted_iota(jnp.int32, (8, size_y), 0)
+        for index in range(slabs):
+            first = index * long
+            x_out[index, plane, :long] = found[first : first + long]
+            x_out[index, plane, long : 2 * long] = found[size_x + first : size_x + first + long]
+            above, under = tiles[(index + 1) % slabs], tiles[(index - 1) % slabs]
+            for pair in range(2):
+                part = slice(8 * pair, 8 * pair + 8)
+                here = slice(8 * index, 8 * index + 8)
+                local = jnp.where(row % 4 < 2, above[part], under[part]) - tiles[index][part]
+                lower = jumps[here, 2 * pair * size_y : (2 * pair + 1) * size_y]
+                upper = jumps[here, (2 * pair + 1) * size_y : (2 * pair + 2) * size_y]
+                start = 2 * long + 8 * pair
+                x_out[index, plane, start : start + 8] = local + jnp.where(row < 4, lower, upper)
+        pltpu.make_async_copy(
+            x_out.at[slab, plane], out.at[slab, plane], own_out.at[plane]
+        ).start()
+        for shift in range(1, slabs):
+            target = (slab + shift) % slabs
+            remote(
+                x_out.at[target, plane], out.at[slab, plane], y_sems, plane, slab_peer(target)
+            ).start()
+
+    stages = (spectrum_stage, pair_stage, sweep_stage, start_stage, return_stage)
+
+    def iteration(time, carry):
+        for delay in reversed(range(len(stages))):
+            plane = time - delay
+
+            @pl.when(jnp.logical_and(plane >= 0, plane < each))
+            def _():
+                stages[delay](plane)
+
+        return carry
+
+    lax.fori_loop(0, each + len(stages) - 1, iteration, 0)
+
+    def finish(plane, carry):
+        await_all(f_send.at[plane], f_sems, 0, plane)
+        await_all(d_send.at[plane], d_sems, 0, plane)
+        if pairs > 1:
+            await_all(c_send.at[pl.ds(0, pairs - 1), plane], c_sems, 0, plane)
+            await_all(s_send.at[pl.ds(0, pairs - 1), plane], s_sems, 0, plane)
+        if slabs > 1:
+            await_all(x_in.at[pl.ds(0, slabs - 1), plane], x_sems, 0, plane)
+            await_all(x_out.at[pl.ds(0, slabs - 1), plane], y_sems, 0, plane)
+            await_all(x_out.at[pl.ds(0, slabs - 1), plane], y_sems, 1, plane)
+        pltpu.make_async_copy(
+            x_out.at[slab, plane], out.at[slab, plane], own_out.at[plane]
+        ).wait()
+        return carry
+
+    lax.fori_loop(0, each, finish, 0)
 
 
 def return_kernel(plan, floats, wave_z, arrived, in_real, in_imag, table, *refs):
@@ -579,7 +718,6 @@
     steps = lax.axis_size("tm")
     slabs = lax.axis_size("space")
     step = lax.axis_index("tm")
-    slab = lax.axis_index("space")
     nodes, long, size_z, size_y = iterate.shape[1:]
     plan = Plan(slabs, steps, long * slabs, size_z, size_y)
     size_x, padded, each = plan.size_x, plan.padded, plan.each
@@ -588,7 +726,6 @@
 
     is_last = (step == steps - 1).astype(jnp.float32)
     floats = jnp.concatenate((velocity, is_last[None]))
-    places = jnp.stack((step, slab)).astype(jnp.int32)
     wave_z = jnp.asarray(plan.z_symbols())
 
     forward = [(index, (index + 1) % slabs) for index in range(slabs)]
@@ -641,51 +778,44 @@
         [floats, wave_z, real.reshape(by_plane), imag.reshape(by_plane)] + tables,
     )
 
-    arrived = lax.all_to_all(
-        sent.reshape(slabs, each, sent_rows, size_y), "space", 0, 0, tiled=True
-    )
-    full_table = plan.symbol_tables(size_x)
-    all_forward = split_constant(plan.x_forward(size_x))
-    all_backward = split_constant(plan.x_backward(size_x))
-    sources = tuple(tripled_constant(matrix) for matrix in plan.jump_sources())
-    slab_block = pl.BlockSpec((slabs, 1, sent_rows, size_y), lambda at: (0, at, 0, 0))
-    step_block = pl.BlockSpec((steps, 1, 2 * own, size_y), lambda at: (0, at, 0, 0))
-    step_shape = shaped(steps, each, 2 * own, size_y)
-    tables = list((full_table,) + all_forward + sources)
-    last = called(
-        functools.partial(last_kernel, plan),
-        "last",
-        (each,),
-        [scalars, scalars, scalars, slab_block] + [whole(table) for table in tables],
-        step_block,
-        step_shape,
-        [floats, wave_z, places, arrived] + tables,
-    )
-
-    gathered = lax.all_to_all(last, "tm", 0, 0, tiled=True)
-    before = called(
-        functools.partial(sweep_kernel, plan),
-        "sweep",
-        (each,),
-        [scalars, scalars, scalars, step_block, whole(full_table)],
-        step_block,
-        step_shape,
-        [floats, wave_z, places, gathered, full_table],
-    )
-    before = lax.all_to_all(before, "tm", 0, 0, tiled=True)
-
-    end_block = pl.BlockSpec((slabs, 1, 16, size_y), lambda at: (0, at, 2 * long // 16, 0))
-    tables = list((full_table,) + all_backward + sources + split_constant(plan.jumps()))
-    back = called(
-        functools.partial(driven_kernel, plan),
-        "driven",
-        (each,),
-        [scalars, scalars, scalars, step_block, end_block] + [whole(table) for table in tables],
-        slab_block,
-        shaped(slabs, each, sent_rows, size_y),
-        [floats, wave_z, places, before, arrived] + tables,
-    )
-    back = lax.all_to_all(back, "space", 0, 0, tiled=True).reshape(padded, sent_rows, size_y)
+    tables = [plan.symbol_tables(size_x)] + list(split_constant(plan.x_forward(size_x)))
+    tables += [tripled_constant(matrix) for matrix in plan.jump_sources()]
+    tables += list(split_constant(plan.x_backward(size_x)) + split_constant(plan.jumps()))
+    half, pairs = size_x // 2, steps // 2
+    anywhere = pl.BlockSpec(memory_space=pl.ANY)
+
+    def held(*shape):
+        return pltpu.VMEM(shape, jnp.float32)
+
+    halves, parts = (each, 2 * half, size_y), (pairs, each, 2 * own, size_y)
+    both = (each, 2, 2 * half, size_y)
+    slots = (slabs, each, sent_rows, size_y)
+    back = pl.pallas_call(
+        functools.partial(spread, plan),
+        name="spread",
+        in_specs=[scalars, scalars, anywhere]
+        + [pl.BlockSpec(memory_space=pltpu.VMEM) for table in tables],
+        out_specs=anywhere,
+        out_shape=shaped(*slots),
+        scratch_shapes=[
+            held(*slots),
+            held(*halves),
+            held(*both),
+            held(*halves),
+            held(*parts),
+            held(*parts),
+            held(*parts),
+            held(*parts),
+            held(*halves),
+            held(*both),
+            held(*slots),
+        ]
+        + [pltpu.SemaphoreType.DMA((2, each))] * 6
+        + [pltpu.SemaphoreType.DMA, pltpu.SemaphoreType.DMA((each,))],
+        compiler_params=pltpu.CompilerParams(
+            collective_id=0, has_side_effects=True, vmem_limit_bytes=56 * 1024 * 1024
+        ),
+    )(floats, wave_z, sent, *tables).reshape(padded, sent_rows, size_y)
 
     ends = tuple(tripled_constant(matrix) for matrix in plan.end_sources())
     tables = list((local_table,) + x_forward + ends + x_backward)

time: 361 us -> 236 us (0.65)
  blocking collectives: 150 us -> 0 us
  Pallas kernels: 163 us -> 223 us
  waiting for transfers between devices: 33.2 us -> 4.98 us
  starting transfers between devices: 6.94 us -> 3.11 us
    all_to_all x3 -> x0, blocking collectives: 150 us -> none  [the longest x1 58 us: shards(): gathered = lax.all_to_all(last, 'tm', 0, 0, tiled=True)]
    pallas_call x0 -> x1, Pallas kernels: none -> 104 us  [shards(): pl.pallas_call(functools.partial(spread, plan), name='spread', in_specs=[...]
    pallas_call x7 -> x4, Pallas kernels: 163 us -> 120 us  [called(): pl.pallas_call(kernel, name=name, grid=grid, in_specs=in_specs, out_specs...]
    all_to_all x1 -> x0, waiting for transfers between devices: 28.3 us -> none  [shards(): lax.all_to_all(sent.reshape(slabs, each, sent_rows, size_y), 'space', 0,...]
    all_to_all x1 -> x0, starting transfers between devices: 3.83 us -> none  [shards(): lax.all_to_all(sent.reshape(slabs, each, sent_rows, size_y), 'space', 0,...]
  transfers between devices with their start and end apart: 3 -> 2, of which waited for: 3 -> 2; matrix products, arithmetic and copies ran while one was open for 1% -> 1% of each run, Pallas kernels for 0% -> 0%
where the time goes in v1:
time: 236 us; the launch traced here: 234 us
  Pallas kernels  223 us (94%)
  waiting for transfers between devices  4.98 us (2%)
  starting transfers between devices  3.11 us (1%)
    pallas_call x4, Pallas kernels, called(): pl.pallas_call(kernel, name=name, grid=grid, in_specs=in_specs, out_specs...  120 us
    pallas_call x1, Pallas kernels, shards(): pl.pallas_call(functools.partial(spread, plan), name='spread', in_specs=[...  104 us
  transfers between devices with their start and end apart: 2, of which 2 were waited for; matrix products, arithmetic and copies ran while one was open for 1% of the time, Pallas kernels for 0%

profile of v1, /device:TPU:0, one launch (start us, length us, event | category | flops | bytes accessed | tf_op | source)
XLA Modules:
  0.0 234.1 jit_solution(5440053101543175644)
XLA Ops:
  0.0 1.0 fusion
  1.0 3.0 %collective-permute-start.1 = (f32[4,1,64,128]{3,2,1,0:T(8,128)S(1)}, f32[4,1,64,128]{3,2,1,0:T(8,128)S(1)}, u32[]{:S(2)}, u32[]{:S(2)}) collective-permute-start(f32[4,1,64,128]{3,2,1,0:T(8,128)S(1)} %get-tuple-element.19), channel_id=1, source_target_pairs={{1,0},{0,1},{3,2},{2,3},{5,4},{4,5},{7,6},{6,7},{9,8},{8,9},{11,10... | collective-permute-start | bytes 393224 | tf_op jit(solution)/shard_map/ppermute | solution.py:734
  4.0 0.1 collective-permute-start
  4.1 1.2 pad_maximum_fusion.floats
  5.3 3.0 %collective-permute-done.1.high_halo = f32[4,1,64,128]{3,2,1,0:T(8,128)S(1)} collective-permute-done((f32[4,1,64,128]{3,2,1,0:T(8,128)S(1)}, f32[4,1,64,128]{3,2,1,0:T(8,128)S(1)}, u32[]{:S(2)}, u32[]{:S(2)}) %collective-permute-start.1) | collective-permute-done | bytes 131104 | tf_op jit(solution)/shard_map/ppermute | solution.py:734
  8.4 0.0 copy-start
  8.4 2.0 collective-permute-done.low_halo
  10.3 0.0 copy-start.1
  10.3 0.0 copy-done
  10.3 0.6 copy-done.1
  11.0 34.1 %enter.1 = (f32[8,1088,128]{2,1,0:T(8,128)}, f32[8,1088,128]{2,1,0:T(8,128)}) custom-call(f32[4]{0:T(128)} %pad_maximum_fusion.floats, f32[4,64,64,128]{3,2,1,0:T(8,128)} %bitcast.10, f32[4,64,64,128]{3,2,1,0:T(8,128)} %bitcast.11, f32[4,64,64,128]{3,2,1,0:T(8,128)} %bitcast.12, f32[4,1,64,128]{3,2,1,0:T(8,128)} %copy-done.1, f32[4,1,64,128]{3,2,1,0:T(8,128)} %copy-done, ...), custom_call_target="tpu_custom_call" | custom-call | tf_op jit(solution)/shard_map/enter/pallas_call | solution.py:699
  45.1 27.8 %modes.1 = (f32[34,4,64,128]{3,2,1,0:T(8,128)}, f32[34,4,64,128]{3,2,1,0:T(8,128)}, f32[34,144,128]{2,1,0:T(8,128)}) custom-call(f32[4]{0:T(128)} %pad_maximum_fusion.floats, f32[2,34]{1,0:T(2,128)} %constant.64.clone.wave_z, f32[8,4,34,8,128]{4,3,2,1,0:T(8,128)} %bitcast.18, f32[8,4,34,8,128]{4,3,2,1,0:T(8,128)} %bitcast.19, ...), custom_call_target="tpu_custom_call" | custom-call | tf_op jit(solution)/shard_map/modes/pallas_call | solution.py:699
  72.9 103.5 %spread.1 = f32[2,17,144,128]{3,2,1,0:T(8,128)} custom-call(f32[4]{0:T(128)} %pad_maximum_fusion.floats, f32[2,34]{1,0:T(2,128)} %constant.64.clone.wave_z, f32[34,144,128]{2,1,0:T(8,128)} %get-tuple-element.14.refs_0_, f32[3,128,128]{2,1,0:T(8,128)} %constant.76.clone.refs_1_, bf16[256,256]{1,0:T(8,128)(2,1)} %constant.77.clone.refs_2_, ...), custom_call_target="tpu_custom_call" | custom-call | tf_op jit(solution)/shard_map/spread/pallas_call | solution.py:793
  176.4 30.4 %return.1 = (f32[8,4,34,8,128]{4,3,2,1,0:T(8,128)}, f32[8,4,34,8,128]{4,3,2,1,0:T(8,128)}) custom-call(f32[4]{0:T(128)} %pad_maximum_fusion.floats, f32[2,34]{1,0:T(2,128)} %constant.64.clone.wave_z, f32[34,144,128]{2,1,0:T(8,128)} %bitcast.14, f32[34,4,64,128]{3,2,1,0:T(8,128)} %get-tuple-element.15.in_real, f32[34,4,64,128]{3,2,1,0:T(8,128)} %get-tuple-element.16.in_imag, ...), custom_call_target="tpu_custom_call" | custom-call | tf_op jit(solution)/shard_map/return/pallas_call | solution.py:699
  206.8 27.3 %leave.1 = f32[4,64,64,128]{3,2,1,0:T(8,128)} custom-call(f32[4]{0:T(128)} %pad_maximum_fusion.floats, f32[8,1088,128]{2,1,0:T(8,128)} %bitcast.16, f32[8,1088,128]{2,1,0:T(8,128)} %bitcast.17, f32[4,64,64,128]{3,2,1,0:T(8,128)} %bitcast.13, bf16[256,256]{1,0:T(8,128)(2,1)} %constant.87.clone.y_high, bf16[256,256]{1,0:T(8,128)(2,1)} %constant.88.clone.y_low, ...), custom_call_target="tpu_custom_call" | custom-call | tf_op jit(solution)/shard_map/leave/pallas_call | solution.py:699
Async XLA Ops:
  1.0 7.4 %collective-permute-start.1 = (f32[4,1,64,128]{3,2,1,0:T(8,128)S(1)}, f32[4,1,64,128]{3,2,1,0:T(8,128)S(1)}, u32[]{:S(2)}, u32[]{:S(2)}) collective-permute-start(f32[4,1,64,128]{3,2,1,0:T(8,128)S(1)} %get-tuple-element.19), channel_id=1, source_target_pairs={{1,0},{0,1},{3,2},{2,3},{5,4},{4,5},{7,6},{6,7},{9,8},{8,9},{11,10... | collective-permute-start | bytes 393224 | tf_op jit(solution)/shard_map/ppermute | solution.py:734
  4.0 6.3 %collective-permute-start = (f32[4,1,64,128]{3,2,1,0:T(8,128)S(1)}, f32[4,1,64,128]{3,2,1,0:T(8,128)S(1)}, u32[]{:S(2)}, u32[]{:S(2)}) collective-permute-start(f32[4,1,64,128]{3,2,1,0:T(8,128)S(1)} %get-tuple-element.20), channel_id=1, source_target_pairs={{0,1},{1,0},{2,3},{3,2},{4,5},{5,4},{6,7},{7,6},{8,9},{9,8},{10,11... | collective-permute-start | bytes 393224 | tf_op jit(solution)/shard_map/ppermute | solution.py:733
  8.4 2.0 copy-start
  10.3 0.7 copy-start.1

commit v2 on v1

--- a/solution.py
+++ b/solution.py
@@ -310,7 +310,7 @@
 
 
 def enter_kernel(plan, floats, it, below, above, low_halo, high_halo, right, diff, *refs):
-    z_high, z_low, y_high, y_low, out_real, out_imag, buffer = refs
+    z_high, z_low, y_high, y_low, out, buffer = refs
     block, rows, size_y = plan.block, plan.rows, plan.size_y
     at = pl.program_id(0)
     first, last = at == 0, at == pl.num_programs(0) - 1
@@ -359,41 +359,11 @@
         for offset in range(2):
             part = along_y[offset * rows : (offset + 1) * rows]
             where = pl.ds(plane + offset, rows, stride=block)
-            out_real[0, where, :] = part[:, :size_y]
-            out_imag[0, where, :] = part[:, size_y:]
+            out[0, 0, where, :] = part[:, :size_y]
+            out[1, 0, where, :] = part[:, size_y:]
         return carry
 
     lax.fori_loop(0, block // 2, pair, 0)
-
-
-def modes_kernel(plan, floats, wave_z, in_real, in_imag, table, *refs):
-    f_high, f_low, b_high, b_low, e_high, e_low, out_real, out_imag, sent = refs
-    long, size_y = plan.long, plan.size_y
-    plane = pl.program_id(0)
-    real = [in_real[:, mode, 0].reshape(long, size_y) for mode in range(4)]
-    imag = [in_imag[:, mode, 0].reshape(long, size_y) for mode in range(4)]
-    value = jnp.concatenate(
-        (jnp.concatenate(real, axis=1), jnp.concatenate(imag, axis=1)), axis=0
-    )
-    spectrum = table_times(f_high[...], f_low[...], value)
-    a_real, a_imag = symbol(table, floats, wave_z, plane)
-    total, inner = None, []
-    for mode in range(4):
-        lanes = slice(mode * size_y, (mode + 1) * size_y)
-        part = (spectrum[:long, lanes], spectrum[long:, lanes])
-        out_real[0, mode], out_imag[0, mode] = part
-        part = times(damped_by(a_real, a_imag, complex(plan.values[mode])), part)
-        total = part if total is None else plus(total, part)
-        inner.append(jnp.concatenate(part, axis=0))
-    last = table_times(b_high[...], b_low[...], jnp.concatenate(total, axis=0))
-    sent[0, : 2 * long] = last
-    ends = table_times(e_high[...], e_low[...], jnp.concatenate(inner, axis=1))[:8]
-    upper = lax.broadcasted_iota(jnp.int32, (8, size_y), 0) < 4
-    for pair in range(2):
-        even = ends[:, 2 * pair * size_y : (2 * pair + 1) * size_y]
-        odd = ends[:, (2 * pair + 1) * size_y : (2 * pair + 2) * size_y]
-        start = 2 * long + 8 * pair
-        sent[0, start : start + 8] = jnp.where(upper, even, odd)
 
 
 def end_spectra(plan, floats, tiles, even, odd):
@@ -413,9 +383,11 @@
 
 
 def spread(plan, floats, wave_z, *refs):
-    (sent, table, f_high, f_low, even, odd, b_high, b_low, j_high, j_low, out) = refs[:11]
-    (x_in, f_send, f_all, growth, c_send, c_all, s_send, s_all, d_send, d_all, x_out) = refs[11:22]
-    (x_sems, f_sems, c_sems, s_sems, d_sems, y_sems, own_in, own_out) = refs[22:]
+    (given, table, f_high, f_low, even, odd, b_high, b_low, j_high, j_low) = refs[:10]
+    (local, lf_high, lf_low, lb_high, lb_low, e_high, e_low, end_even, end_odd, out) = refs[10:20]
+    (held, sent, x_in, f_send, f_all, growth, c_send, c_all, s_send) = refs[20:29]
+    (s_all, d_send, d_all, x_out, y_in) = refs[29:34]
+    (x_sems, f_sems, c_sems, s_sems, d_sems, y_sems, in_sems, out_sems) = refs[34:]
     slabs, steps, each = plan.slabs, plan.steps, plan.each
     long, size_x, size_y, own = plan.long, plan.size_x, plan.size_y, plan.own_x
     half, pairs = size_x // 2, steps // 2
@@ -450,23 +422,99 @@
     def await_all(ref, sems, kind, plane):
         pltpu.make_async_copy(ref, ref, sems.at[kind, plane]).wait()
 
-    mine = pltpu.make_async_copy(sent.at[pl.ds(slab * each, each)], x_in.at[slab], own_in)
-    mine.start()
-
-    def start_plane(plane, carry):
+    def fetch(plane):
+        return pltpu.make_async_copy(given.at[:, :, :, plane], held.at[plane], in_sems.at[plane])
+
+    def write(plane):
+        return pltpu.make_async_copy(held.at[plane], out.at[:, :, :, plane], out_sems.at[plane])
+
+    def fetch_all(plane, carry):
+        for index in range(slabs):
+            fetch(index * each + plane).start()
+        return carry
+
+    lax.fori_loop(0, each, fetch_all, 0)
+
+    def local_mode(index):
+        return slice(index * size_y, (index + 1) * size_y)
+
+    def modes_of(plane, index):
+        at = index * each + plane
+        fetch(at).wait()
+        parts = [
+            jnp.concatenate(
+                [held[at, part, :, mode].reshape(long, size_y) for mode in range(4)], axis=1
+            )
+            for part in range(2)
+        ]
+        spectrum = table_times(lf_high[...], lf_low[...], jnp.concatenate(parts, axis=0))
+        a_real, a_imag = symbol(local, floats, wave_z, at)
+        total, inner = None, []
+        shape = (plan.blocks, plan.block, size_y)
+        for mode in range(4):
+            part = (spectrum[:long, local_mode(mode)], spectrum[long:, local_mode(mode)])
+            held[at, 0, :, mode] = part[0].reshape(shape)
+            held[at, 1, :, mode] = part[1].reshape(shape)
+            part = times(damped_by(a_real, a_imag, complex(plan.values[mode])), part)
+            total = part if total is None else plus(total, part)
+            inner.append(jnp.concatenate(part, axis=0))
+        sent[index, plane, : 2 * long] = table_times(
+            lb_high[...], lb_low[...], jnp.concatenate(total, axis=0)
+        )
+        ends = table_times(e_high[...], e_low[...], jnp.concatenate(inner, axis=1))[:8]
+        upper = lax.broadcasted_iota(jnp.int32, (8, size_y), 0) < 4
+        for pair in range(2):
+            start = 2 * long + 8 * pair
+            sent[index, plane, start : start + 8] = jnp.where(
+                upper, ends[:, local_mode(2 * pair)], ends[:, local_mode(2 * pair + 1)]
+            )
+
+    def modes_stage(plane):
+        targets = [(slab + shift) % slabs for shift in range(1, slabs)]
+        for target in targets:
+            modes_of(plane, target)
+        for target in targets:
+            remote(
+                sent.at[target, plane], x_in.at[slab, plane], x_sems, plane, slab_peer(target)
+            ).start()
+        modes_of(plane, slab)
+        x_in[slab, plane] = sent[slab, plane]
+
+    def solution_of(plane, index):
+        at = index * each + plane
+        found = table_times(lf_high[...], lf_low[...], y_in[index, plane, : 2 * long])
+        before = (found[:long], found[long:])
+        start = 2 * long
+        ends = jnp.concatenate(
+            (y_in[index, plane, start : start + 8], y_in[index, plane, start + 8 :]), axis=1
+        )
+        value = tripled(ends * end_scale(floats, ends.shape))
+        sources = [dot(end_even[...], value), dot(end_odd[...], value)]
+        a_real, a_imag = symbol(local, floats, wave_z, at)
+        driven = []
+        for mode in range(4):
+            source = sources[mode % 2][:, local_mode(mode // 2)]
+            total = times(number(plan.values[mode]), (source[:long], source[long:]))
+            total = plus(total, times(number(plan.weights[mode]), before))
+            kept = [held[at, part, :, mode].reshape(long, size_y) for part in range(2)]
+            total = plus(total, kept)
+            damped = damped_by(a_real, a_imag, complex(plan.values[mode]))
+            driven.append(jnp.concatenate(times(damped, total), axis=0))
+        back = table_times(lb_high[...], lb_low[...], jnp.concatenate(driven, axis=1))
+        shape = (plan.blocks, plan.block, size_y)
+        for mode in range(4):
+            held[at, 0, :, mode] = back[:long, local_mode(mode)].reshape(shape)
+            held[at, 1, :, mode] = back[long:, local_mode(mode)].reshape(shape)
+
+    def solution_stage(plane):
+        solution_of(plane, slab)
+        write(slab * each + plane).start()
+        if slabs > 1:
+            await_all(x_out.at[pl.ds(0, slabs - 1), plane], y_sems, 1, plane)
         for shift in range(1, slabs):
             target = (slab + shift) % slabs
-            remote(
-                sent.at[target * each + plane],
-                x_in.at[slab, plane],
-                x_sems,
-                plane,
-                slab_peer(target),
-            ).start()
-        return carry
-
-    lax.fori_loop(0, each, start_plane, 0)
-    mine.wait()
+            solution_of(plane, target)
+            write(target * each + plane).start()
 
     def symbols(plane, start, count):
         rows = pl.ds(start, count)
@@ -588,20 +636,21 @@
                 upper = jumps[here, (2 * pair + 1) * size_y : (2 * pair + 2) * size_y]
                 start = 2 * long + 8 * pair
                 x_out[index, plane, start : start + 8] = local + jnp.where(row < 4, lower, upper)
-        pltpu.make_async_copy(
-            x_out.at[slab, plane], out.at[slab, plane], own_out.at[plane]
-        ).start()
+        y_in[slab, plane] = x_out[slab, plane]
         for shift in range(1, slabs):
             target = (slab + shift) % slabs
             remote(
-                x_out.at[target, plane], out.at[slab, plane], y_sems, plane, slab_peer(target)
+                x_out.at[target, plane], y_in.at[slab, plane], y_sems, plane, slab_peer(target)
             ).start()
 
-    stages = (spectrum_stage, pair_stage, sweep_stage, start_stage, return_stage)
+    stages = (modes_stage, spectrum_stage, pair_stage, sweep_stage)
+    stages += (start_stage, return_stage, solution_stage)
+
+    delays = (0, 1, 2, 3, 4, 5, 6)
 
     def iteration(time, carry):
         for delay in reversed(range(len(stages))):
-            plane = time - delay
+            plane = time - delays[delay]
 
             @pl.when(jnp.logical_and(plane >= 0, plane < each))
             def _():
@@ -609,7 +658,7 @@
 
         return carry
 
-    lax.fori_loop(0, each + len(stages) - 1, iteration, 0)
+    lax.fori_loop(0, each + delays[-1], iteration, 0)
 
     def finish(plane, carry):
         await_all(f_send.at[plane], f_sems, 0, plane)
@@ -620,43 +669,14 @@
         if slabs > 1:
             await_all(x_in.at[pl.ds(0, slabs - 1), plane], x_sems, 0, plane)
             await_all(x_out.at[pl.ds(0, slabs - 1), plane], y_sems, 0, plane)
-            await_all(x_out.at[pl.ds(0, slabs - 1), plane], y_sems, 1, plane)
-        pltpu.make_async_copy(
-            x_out.at[slab, plane], out.at[slab, plane], own_out.at[plane]
-        ).wait()
+        for index in range(slabs):
+            write(index * each + plane).wait()
         return carry
 
     lax.fori_loop(0, each, finish, 0)
 
 
-def return_kernel(plan, floats, wave_z, arrived, in_real, in_imag, table, *refs):
-    f_high, f_low, even, odd, b_high, b_low, out_real, out_imag = refs
-    long, size_y = plan.long, plan.size_y
-    plane = pl.program_id(0)
-    found = table_times(f_high[...], f_low[...], arrived[0, : 2 * long])
-    before = (found[:long], found[long:])
-    ends = jnp.concatenate((arrived[0, 2 * long : 2 * long + 8], arrived[0, 2 * long + 8 :]), axis=1)
-    value = tripled(ends * end_scale(floats, ends.shape))
-    sources = [dot(even[...], value), dot(odd[...], value)]
-    a_real, a_imag = symbol(table, floats, wave_z, plane)
-    driven = []
-    for mode in range(4):
-        lanes = slice((mode // 2) * size_y, (mode // 2 + 1) * size_y)
-        source = sources[mode % 2][:, lanes]
-        total = times(number(plan.values[mode]), (source[:long], source[long:]))
-        total = plus(total, times(number(plan.weights[mode]), before))
-        total = plus(total, (in_real[0, mode], in_imag[0, mode]))
-        damped = damped_by(a_real, a_imag, complex(plan.values[mode]))
-        driven.append(jnp.concatenate(times(damped, total), axis=0))
-    back = table_times(b_high[...], b_low[...], jnp.concatenate(driven, axis=1))
-    for mode in range(4):
-        lanes = slice(mode * size_y, (mode + 1) * size_y)
-        shape = (plan.blocks, plan.block, size_y)
-        out_real[:, mode, 0] = back[:long, lanes].reshape(shape)
-        out_imag[:, mode, 0] = back[long:, lanes].reshape(shape)
-
-
-def leave_kernel(plan, floats, in_real, in_imag, kept, y_high, y_low, z_high, z_low, z_rest, out):
+def leave_kernel(plan, floats, found_in, kept, y_high, y_low, z_high, z_low, z_rest, out):
     block, rows, size_y, size_z = plan.block, plan.rows, plan.size_y, plan.size_z
     most = z_high.shape[1]
 
@@ -665,7 +685,7 @@
         parts = []
         for offset in range(2):
             where = pl.ds(plane + offset, rows, stride=block)
-            parts.append(jnp.concatenate((in_real[0, where, :], in_imag[0, where, :]), axis=1))
+            parts.append(jnp.concatenate((found_in[0, 0, where, :], found_in[1, 0, where, :]), axis=1))
         along_y = times_table(jnp.concatenate(parts, axis=0), y_high[...], y_low[...])
         stacked = jnp.concatenate(
             (
@@ -738,8 +758,8 @@
     tables = list(z_tables + y_tables)
     thick = pl.BlockSpec((4, block, size_z, size_y), lambda at: (0, at, 0, 0))
     thin = (4, 1, size_z, size_y)
-    out_block = pl.BlockSpec((1, rows * block, size_y), lambda at: (at, 0, 0))
-    real, imag = called(
+    out_block = pl.BlockSpec((2, 1, rows * block, size_y), lambda at: (0, at, 0, 0))
+    spectrum = called(
         functools.partial(enter_kernel, plan),
         "enter",
         (blocks,),
@@ -754,33 +774,19 @@
             pl.BlockSpec((block, size_z, size_y), lambda at: (at, 0, 0)),
         ]
         + [whole(table) for table in tables],
-        [out_block, out_block],
-        [shaped(blocks, rows * block, size_y)] * 2,
+        out_block,
+        shaped(2, blocks, rows * block, size_y),
         [floats, iterate, iterate, iterate, low_halo, high_halo, right_side, diffusivity] + tables,
         scratch=[pltpu.VMEM((4, block + 2, size_z, size_y), jnp.float32)],
     )
 
-    by_plane = (blocks, 4, padded, block, size_y)
-    plane_block = pl.BlockSpec((blocks, 4, 1, block, size_y), lambda at: (0, 0, at, 0, 0))
-    mode_block = pl.BlockSpec((1, 4, long, size_y), lambda at: (at, 0, 0, 0))
-    sent_block = pl.BlockSpec((1, sent_rows, size_y), lambda at: (at, 0, 0))
-    local_table = plan.symbol_tables(long)
-    x_forward = split_constant(plan.x_forward(long))
-    x_backward = split_constant(plan.x_backward(long))
-    tables = list((local_table,) + x_forward + x_backward + split_constant(plan.ends()))
-    mode_real, mode_imag, sent = called(
-        functools.partial(modes_kernel, plan),
-        "modes",
-        (padded,),
-        [scalars, scalars, plane_block, plane_block] + [whole(table) for table in tables],
-        [mode_block, mode_block, sent_block],
-        [shaped(padded, 4, long, size_y)] * 2 + [shaped(padded, sent_rows, size_y)],
-        [floats, wave_z, real.reshape(by_plane), imag.reshape(by_plane)] + tables,
-    )
-
+    by_plane = (2, blocks, 4, padded, block, size_y)
     tables = [plan.symbol_tables(size_x)] + list(split_constant(plan.x_forward(size_x)))
     tables += [tripled_constant(matrix) for matrix in plan.jump_sources()]
     tables += list(split_constant(plan.x_backward(size_x)) + split_constant(plan.jumps()))
+    tables += [plan.symbol_tables(long)] + list(split_constant(plan.x_forward(long)))
+    tables += list(split_constant(plan.x_backward(long)) + split_constant(plan.ends()))
+    tables += [tripled_constant(matrix) for matrix in plan.end_sources()]
     half, pairs = size_x // 2, steps // 2
     anywhere = pl.BlockSpec(memory_space=pl.ANY)
 
@@ -790,14 +796,16 @@
     halves, parts = (each, 2 * half, size_y), (pairs, each, 2 * own, size_y)
     both = (each, 2, 2 * half, size_y)
     slots = (slabs, each, sent_rows, size_y)
-    back = pl.pallas_call(
+    spectrum = pl.pallas_call(
         functools.partial(spread, plan),
         name="spread",
         in_specs=[scalars, scalars, anywhere]
         + [pl.BlockSpec(memory_space=pltpu.VMEM) for table in tables],
         out_specs=anywhere,
-        out_shape=shaped(*slots),
+        out_shape=shaped(*by_plane),
         scratch_shapes=[
+            held(padded, 2, blocks, 4, block, size_y),
+            held(*slots),
             held(*slots),
             held(*halves),
             held(*both),
@@ -809,25 +817,14 @@
             held(*halves),
             held(*both),
             held(*slots),
+            held(*slots),
         ]
         + [pltpu.SemaphoreType.DMA((2, each))] * 6
-        + [pltpu.SemaphoreType.DMA, pltpu.SemaphoreType.DMA((each,))],
+        + [pltpu.SemaphoreType.DMA((padded,))] * 2,
         compiler_params=pltpu.CompilerParams(
             collective_id=0, has_side_effects=True, vmem_limit_bytes=56 * 1024 * 1024
         ),
-    )(floats, wave_z, sent, *tables).reshape(padded, sent_rows, size_y)
-
-    ends = tuple(tripled_constant(matrix) for matrix in plan.end_sources())
-    tables = list((local_table,) + x_forward + ends + x_backward)
-    real, imag = called(
-        functools.partial(return_kernel, plan),
-        "return",
-        (padded,),
-        [scalars, scalars, sent_block, mode_block, mode_block] + [whole(table) for table in tables],
-        [plane_block, plane_block],
-        [shaped(*by_plane)] * 2,
-        [floats, wave_z, back, mode_real, mode_imag] + tables,
-    )
+    )(floats, wave_z, spectrum.reshape(by_plane), *tables)
 
     z_backward = plan.z_backward()
     most = min(256, 2 * rows)
@@ -841,7 +838,6 @@
         [
             scalars,
             out_block,
-            out_block,
             pl.BlockSpec((1, block, size_z, size_y), lambda at: (3, at, 0, 0)),
         ]
         + [whole(table) for table in tables],
@@ -849,8 +845,7 @@
         shaped(4, long, size_z, size_y),
         [
             floats,
-            real.reshape(blocks, rows * block, size_y),
-            imag.reshape(blocks, rows * block, size_y),
+            spectrum.reshape(2, blocks, rows * block, size_y),
             iterate,
         ]
         + tables,

time: 236 us -> 184 us (0.78)
  Pallas kernels: 223 us -> 173 us
    pallas_call x4 -> x2, Pallas kernels: 120 us -> 61.3 us  [called(): pl.pallas_call(kernel, name=name, grid=grid, in_specs=in_specs, out_specs...]
    pallas_call x1, Pallas kernels: 104 us -> 112 us  [shards(): pl.pallas_call(functools.partial(spread, plan), name='spread', in_specs=[...]
where the time goes in v2:
time: 184 us
  Pallas kernels  173 us (94%)
  waiting for transfers between devices  4.99 us (3%)
  starting transfers between devices  3.11 us (2%)
    pallas_call x1, Pallas kernels, shards(): pl.pallas_call(functools.partial(spread, plan), name='spread', in_specs=[...  112 us
    pallas_call x2, Pallas kernels, called(): pl.pallas_call(kernel, name=name, grid=grid, in_specs=in_specs, out_specs...  61.3 us
  transfers between devices with their start and end apart: 2, of which 2 were waited for; matrix products, arithmetic and copies ran while one was open for 1% of the time, Pallas kernels for 0%

profile of v2, /device:TPU:0, one launch (start us, length us, event | category | flops | bytes accessed | tf_op | source)
XLA Modules:
  0.0 184.2 jit_solution(15936542762922056904)
XLA Ops:
  0.0 1.0 fusion
  1.0 3.0 %collective-permute-start.1 = (f32[4,1,64,128]{3,2,1,0:T(8,128)S(1)}, f32[4,1,64,128]{3,2,1,0:T(8,128)S(1)}, u32[]{:S(2)}, u32[]{:S(2)}) collective-permute-start(f32[4,1,64,128]{3,2,1,0:T(8,128)S(1)} %get-tuple-element.5), channel_id=1, source_target_pairs={{1,0},{0,1},{3,2},{2,3},{5,4},{4,5},{7,6},{6,7},{9,8},{8,9},{11,10... | collective-permute-start | bytes 393224 | tf_op jit(solution)/shard_map/ppermute | solution.py:754
  4.0 0.1 collective-permute-start
  4.1 1.2 pad_maximum_fusion.floats
  5.3 3.0 %collective-permute-done.1.high_halo = f32[4,1,64,128]{3,2,1,0:T(8,128)S(1)} collective-permute-done((f32[4,1,64,128]{3,2,1,0:T(8,128)S(1)}, f32[4,1,64,128]{3,2,1,0:T(8,128)S(1)}, u32[]{:S(2)}, u32[]{:S(2)}) %collective-permute-start.1) | collective-permute-done | bytes 131104 | tf_op jit(solution)/shard_map/ppermute | solution.py:754
  8.4 0.0 copy-start
  8.4 2.0 %collective-permute-done.low_halo = f32[4,1,64,128]{3,2,1,0:T(8,128)S(1)} collective-permute-done((f32[4,1,64,128]{3,2,1,0:T(8,128)S(1)}, f32[4,1,64,128]{3,2,1,0:T(8,128)S(1)}, u32[]{:S(2)}, u32[]{:S(2)}) %collective-permute-start) | collective-permute-done | bytes 131104 | tf_op jit(solution)/shard_map/ppermute | solution.py:753
  10.3 0.0 copy-start.1
  10.3 0.0 copy-done
  10.3 0.7 copy-done.1
  11.0 34.1 %enter.1 = f32[2,8,1088,128]{3,2,1,0:T(8,128)} custom-call(f32[4]{0:T(128)} %pad_maximum_fusion.floats, f32[4,64,64,128]{3,2,1,0:T(8,128)} %bitcast.7, f32[4,64,64,128]{3,2,1,0:T(8,128)} %bitcast.8, f32[4,64,64,128]{3,2,1,0:T(8,128)} %bitcast.9, f32[4,1,64,128]{3,2,1,0:T(8,128)} %copy-done.1, f32[4,1,64,128]{3,2,1,0:T(8,128)} %copy-done, ...), custom_call_target="tpu_custom_call" | custom-call | tf_op jit(solution)/shard_map/enter/pallas_call | solution.py:719
  45.1 112.0 %spread.1 = f32[2,8,4,34,8,128]{5,4,3,2,1,0:T(8,128)} custom-call(f32[4]{0:T(128)} %pad_maximum_fusion.floats, f32[2,34]{1,0:T(2,128)} %constant.64.clone.wave_z, f32[2,8,4,34,8,128]{5,4,3,2,1,0:T(8,128)} %bitcast.11, f32[3,128,128]{2,1,0:T(8,128)} %constant.69.clone.refs_1_, bf16[256,256]{1,0:T(8,128)(2,1)} %constant.70.clone.refs_2_, ...), custom_call_target="tpu_custom_call" | custom-call | tf_op jit(solution)/shard_map/spread/pallas_call | solution.py:799
  157.1 27.1 %leave.1 = f32[4,64,64,128]{3,2,1,0:T(8,128)} custom-call(f32[4]{0:T(128)} %pad_maximum_fusion.floats, f32[2,8,1088,128]{3,2,1,0:T(8,128)} %bitcast.12, f32[4,64,64,128]{3,2,1,0:T(8,128)} %bitcast.10, bf16[256,256]{1,0:T(8,128)(2,1)} %constant.87.clone.y_high, bf16[256,256]{1,0:T(8,128)(2,1)} %constant.88.clone.y_low, ...), custom_call_target="tpu_custom_call" | custom-call | tf_op jit(solution)/shard_map/leave/pallas_call | solution.py:719
Async XLA Ops:
  1.0 7.4 %collective-permute-start.1 = (f32[4,1,64,128]{3,2,1,0:T(8,128)S(1)}, f32[4,1,64,128]{3,2,1,0:T(8,128)S(1)}, u32[]{:S(2)}, u32[]{:S(2)}) collective-permute-start(f32[4,1,64,128]{3,2,1,0:T(8,128)S(1)} %get-tuple-element.5), channel_id=1, source_target_pairs={{1,0},{0,1},{3,2},{2,3},{5,4},{4,5},{7,6},{6,7},{9,8},{8,9},{11,10... | collective-permute-start | bytes 393224 | tf_op jit(solution)/shard_map/ppermute | solution.py:754
  4.0 6.3 %collective-permute-start = (f32[4,1,64,128]{3,2,1,0:T(8,128)S(1)}, f32[4,1,64,128]{3,2,1,0:T(8,128)S(1)}, u32[]{:S(2)}, u32[]{:S(2)}) collective-permute-start(f32[4,1,64,128]{3,2,1,0:T(8,128)S(1)} %get-tuple-element.6), channel_id=1, source_target_pairs={{0,1},{1,0},{2,3},{3,2},{4,5},{5,4},{6,7},{7,6},{8,9},{9,8},{10,11... | collective-permute-start | bytes 393224 | tf_op jit(solution)/shard_map/ppermute | solution.py:753
  8.4 2.0 %copy-start = (f32[4,1,64,128]{3,2,1,0:T(8,128)}, f32[4,1,64,128]{3,2,1,0:T(8,128)S(1)}, u32[]{:S(2)}) copy-start(f32[4,1,64,128]{3,2,1,0:T(8,128)S(1)} %collective-permute-done.1.high_halo) | copy-start | bytes 393220
  10.3 0.7 copy-start.1

commit v3 on v2

--- a/solution.py
+++ b/solution.py
@@ -309,14 +309,52 @@
     return jnp.where(row < 2, upper, lower)
 
 
-def enter_kernel(plan, floats, it, below, above, low_halo, high_halo, right, diff, *refs):
-    z_high, z_low, y_high, y_low, out, buffer = refs
-    block, rows, size_y = plan.block, plan.rows, plan.size_y
-    at = pl.program_id(0)
-    first, last = at == 0, at == pl.num_programs(0) - 1
+def enter_kernel(plan, floats, it, below, above, right, diff, field, *refs):
+    z_high, z_low, y_high, y_low, out, buffer, halo, sends, receives = refs
+    block, rows, size_y, slabs = plan.block, plan.rows, plan.size_y, plan.slabs
+    count = plan.blocks
+    turn = pl.program_id(0)
+    at = (turn + 1) % count
+    step, slab = lax.axis_index("tm"), lax.axis_index("space")
+    upper_slab, lower_slab = (step, (slab + 1) % slabs), (step, (slab + slabs - 1) % slabs)
+
+    def edge(index):
+        plane = (plan.long - 1, 0)[index]
+        return pltpu.make_async_remote_copy(
+            src_ref=field.at[:, pl.ds(plane, 1)],
+            dst_ref=halo.at[index],
+            send_sem=sends.at[index],
+            recv_sem=receives.at[index],
+            device_id=(upper_slab, lower_slab)[index],
+            device_id_type=MESH,
+        )
+
+    @pl.when(turn == 0)
+    def _():
+        barrier = pltpu.get_barrier_semaphore()
+        for device in (upper_slab, lower_slab):
+            pl.semaphore_signal(barrier, inc=1, device_id=device, device_id_type=MESH)
+        pl.semaphore_wait(barrier, 2)
+        for index in range(2):
+            edge(index).start()
+
+    @pl.when(turn == max(count - 2, 0))
+    def _():
+        for index in range(2):
+            edge(index).wait()
+
     buffer[:, 1 : block + 1] = it[...]
-    buffer[:, 0:1] = jnp.where(first, low_halo[...], below[...])
-    buffer[:, block + 1 :] = jnp.where(last, high_halo[...], above[...])
+    buffer[:, 0:1] = below[...]
+    buffer[:, block + 1 :] = above[...]
+
+    @pl.when(at == 0)
+    def _():
+        buffer[:, 0:1] = halo[0]
+
+    @pl.when(at == count - 1)
+    def _():
+        buffer[:, block + 1 :] = halo[1]
+
     nodes = plan.matrix.sum(axis=1)
     size_z = plan.size_z
 
@@ -363,7 +401,7 @@
             out[1, 0, where, :] = part[:, size_y:]
         return carry
 
-    lax.fori_loop(0, block // 2, pair, 0)
+    lax.fori_loop(0, block // 2, pair, 0, unroll=4)
 
 
 def end_spectra(plan, floats, tiles, even, odd):
@@ -438,16 +476,18 @@
     def local_mode(index):
         return slice(index * size_y, (index + 1) * size_y)
 
-    def modes_of(plane, index):
+    def spectrum_of(plane, index):
         at = index * each + plane
-        fetch(at).wait()
         parts = [
             jnp.concatenate(
                 [held[at, part, :, mode].reshape(long, size_y) for mode in range(4)], axis=1
             )
             for part in range(2)
         ]
-        spectrum = table_times(lf_high[...], lf_low[...], jnp.concatenate(parts, axis=0))
+        return table_times(lf_high[...], lf_low[...], jnp.concatenate(parts, axis=0))
+
+    def modes_of(plane, index, spectrum):
+        at = index * each + plane
         a_real, a_imag = symbol(local, floats, wave_z, at)
         total, inner = None, []
         shape = (plan.blocks, plan.block, size_y)
@@ -471,14 +511,16 @@
 
     def modes_stage(plane):
         targets = [(slab + shift) % slabs for shift in range(1, slabs)]
-        for target in targets:
-            modes_of(plane, target)
+        for index in range(slabs):
+            fetch(index * each + plane).wait()
+        spectra = [spectrum_of(plane, index) for index in range(slabs)]
+        for index in range(slabs):
+            modes_of(plane, index, spectra[index])
+        x_in[slab, plane] = sent[slab, plane]
         for target in targets:
             remote(
                 sent.at[target, plane], x_in.at[slab, plane], x_sems, plane, slab_peer(target)
             ).start()
-        modes_of(plane, slab)
-        x_in[slab, plane] = sent[slab, plane]
 
     def solution_of(plane, index):
         at = index * each + plane
@@ -500,21 +542,24 @@
             total = plus(total, kept)
             damped = damped_by(a_real, a_imag, complex(plan.values[mode]))
             driven.append(jnp.concatenate(times(damped, total), axis=0))
-        back = table_times(lb_high[...], lb_low[...], jnp.concatenate(driven, axis=1))
+        return jnp.concatenate(driven, axis=1)
+
+    def keep_solution(plane, index, driven):
+        at = index * each + plane
+        back = table_times(lb_high[...], lb_low[...], driven)
         shape = (plan.blocks, plan.block, size_y)
         for mode in range(4):
             held[at, 0, :, mode] = back[:long, local_mode(mode)].reshape(shape)
             held[at, 1, :, mode] = back[long:, local_mode(mode)].reshape(shape)
 
     def solution_stage(plane):
-        solution_of(plane, slab)
-        write(slab * each + plane).start()
         if slabs > 1:
             await_all(x_out.at[pl.ds(0, slabs - 1), plane], y_sems, 1, plane)
-        for shift in range(1, slabs):
-            target = (slab + shift) % slabs
-            solution_of(plane, target)
-            write(target * each + plane).start()
+        driven = [solution_of(plane, index) for index in range(slabs)]
+        for index in range(slabs):
+            keep_solution(plane, index, driven[index])
+        for index in range(slabs):
+            write(index * each + plane).start()
 
     def symbols(plane, start, count):
         rows = pl.ds(start, count)
@@ -649,7 +694,7 @@
     delays = (0, 1, 2, 3, 4, 5, 6)
 
     def iteration(time, carry):
-        for delay in reversed(range(len(stages))):
+        for delay in range(len(stages)):
             plane = time - delays[delay]
 
             @pl.when(jnp.logical_and(plane >= 0, plane < each))
@@ -704,7 +749,7 @@
                 out[node, plane + offset] = part[:, offset * size_y : (offset + 1) * size_y] + add
         return carry
 
-    lax.fori_loop(0, block // 2, pair, 0)
+    lax.fori_loop(0, block // 2, pair, 0, unroll=4)
 
 
 def whole(array):
@@ -715,7 +760,7 @@
 scalars = pl.BlockSpec(memory_space=pltpu.SMEM)
 
 
-def called(kernel, name, grid, in_specs, out_specs, out_shape, operands, flops=0, scratch=()):
+def called(kernel, name, grid, in_specs, out_specs, out_shape, operands, scratch=(), collective=None):
     return pl.pallas_call(
         kernel,
         name=name,
@@ -725,7 +770,10 @@
         out_shape=out_shape,
         scratch_shapes=list(scratch),
         compiler_params=pltpu.CompilerParams(
-            dimension_semantics=("arbitrary",) * len(grid), vmem_limit_bytes=56 * 1024 * 1024
+            dimension_semantics=("arbitrary",) * len(grid),
+            vmem_limit_bytes=56 * 1024 * 1024,
+            collective_id=collective,
+            has_side_effects=collective is not None,
         ),
     )(*operands)
 
@@ -748,36 +796,41 @@
     floats = jnp.concatenate((velocity, is_last[None]))
     wave_z = jnp.asarray(plan.z_symbols())
 
-    forward = [(index, (index + 1) % slabs) for index in range(slabs)]
-    backward = [(target, source) for source, target in forward]
-    low_halo = lax.ppermute(iterate[:, -1:], "space", forward)
-    high_halo = lax.ppermute(iterate[:, :1], "space", backward)
-
     z_tables = split_constant(plan.z_forward())
     y_tables = split_constant(plan.y_forward())
     tables = list(z_tables + y_tables)
-    thick = pl.BlockSpec((4, block, size_z, size_y), lambda at: (0, at, 0, 0))
     thin = (4, 1, size_z, size_y)
-    out_block = pl.BlockSpec((2, 1, rows * block, size_y), lambda at: (0, at, 0, 0))
+    anywhere = pl.BlockSpec(memory_space=pl.ANY)
+
+    def turned(at):
+        return (at + 1) % blocks
+
     spectrum = called(
         functools.partial(enter_kernel, plan),
         "enter",
         (blocks,),
         [
             scalars,
-            thick,
-            pl.BlockSpec(thin, lambda at: (0, jnp.maximum(at * block - 1, 0), 0, 0)),
-            pl.BlockSpec(thin, lambda at: (0, jnp.minimum(at * block + block, long - 1), 0, 0)),
-            whole(low_halo),
-            whole(high_halo),
-            thick,
-            pl.BlockSpec((block, size_z, size_y), lambda at: (at, 0, 0)),
+            pl.BlockSpec((4, block, size_z, size_y), lambda at: (0, turned(at), 0, 0)),
+            pl.BlockSpec(thin, lambda at: (0, jnp.maximum(turned(at) * block - 1, 0), 0, 0)),
+            pl.BlockSpec(
+                thin, lambda at: (0, jnp.minimum(turned(at) * block + block, long - 1), 0, 0)
+            ),
+            pl.BlockSpec((4, block, size_z, size_y), lambda at: (0, turned(at), 0, 0)),
+            pl.BlockSpec((block, size_z, size_y), lambda at: (turned(at), 0, 0)),
+            anywhere,
         ]
         + [whole(table) for table in tables],
-        out_block,
+        pl.BlockSpec((2, 1, rows * block, size_y), lambda at: (0, turned(at), 0, 0)),
         shaped(2, blocks, rows * block, size_y),
-        [floats, iterate, iterate, iterate, low_halo, high_halo, right_side, diffusivity] + tables,
-        scratch=[pltpu.VMEM((4, block + 2, size_z, size_y), jnp.float32)],
+        [floats, iterate, iterate, iterate, right_side, diffusivity, iterate] + tables,
+        scratch=[
+            pltpu.VMEM((4, block + 2, size_z, size_y), jnp.float32),
+            pltpu.VMEM((2,) + thin, jnp.float32),
+            pltpu.SemaphoreType.DMA((2,)),
+            pltpu.SemaphoreType.DMA((2,)),
+        ],
+        collective=1,
     )
 
     by_plane = (2, blocks, 4, padded, block, size_y)
@@ -788,7 +841,6 @@
     tables += list(split_constant(plan.x_backward(long)) + split_constant(plan.ends()))
     tables += [tripled_constant(matrix) for matrix in plan.end_sources()]
     half, pairs = size_x // 2, steps // 2
-    anywhere = pl.BlockSpec(memory_space=pl.ANY)
 
     def held(*shape):
         return pltpu.VMEM(shape, jnp.float32)
@@ -837,11 +889,11 @@
         (blocks,),
         [
             scalars,
-            out_block,
+            pl.BlockSpec((2, 1, rows * block, size_y), lambda at: (0, at, 0, 0)),
             pl.BlockSpec((1, block, size_z, size_y), lambda at: (3, at, 0, 0)),
         ]
         + [whole(table) for table in tables],
-        thick,
+        pl.BlockSpec((4, block, size_z, size_y), lambda at: (0, at, 0, 0)),
         shaped(4, long, size_z, size_y),
         [
             floats,

time: 184 us -> 136 us (0.74)
  Pallas kernels: 173 us -> 134 us
  waiting for transfers between devices: 4.99 us -> 0 us
  starting transfers between devices: 3.11 us -> 0 us
    pallas_call x2, Pallas kernels: 61.3 us -> 40.2 us  [called(): pl.pallas_call(kernel, name=name, grid=grid, in_specs=in_specs, out_specs...]
    pallas_call x1, Pallas kernels: 112 us -> 94 us  [shards(): pl.pallas_call(functools.partial(spread, plan), name='spread', in_specs=[...]
    ppermute x2 -> x0, waiting for transfers between devices: 4.99 us -> none  [the longest x1 3.04 us: shards(): high_halo = lax.ppermute(iterate[:, :1], 'space', backward)]
    ppermute x2 -> x0, starting transfers between devices: 3.11 us -> none  [the longest x1 3.03 us: shards(): high_halo = lax.ppermute(iterate[:, :1], 'space', backward)]
  transfers between devices with their start and end apart: 2 -> 0, of which waited for: 2 -> 0; matrix products, arithmetic and copies ran while one was open for 1% -> 0% of each run, Pallas kernels for 0% -> 0%
where the time goes in v3:
time: 136 us; the launch traced here: 135 us
  Pallas kernels  134 us (99%)
    pallas_call x1, Pallas kernels, shards(): pl.pallas_call(functools.partial(spread, plan), name='spread', in_specs=[...  94 us
    pallas_call x2, Pallas kernels, called(): pl.pallas_call(kernel, name=name, grid=grid, in_specs=in_specs, out_specs...  40.2 us

profile of v3, /device:TPU:0, one launch (start us, length us, event | category | flops | bytes accessed | tf_op | source)
XLA Modules:
  0.0 135.4 jit_solution(9625459511133889134)
XLA Ops:
  0.0 1.2 pad_maximum_fusion.floats
  1.2 22.9 %enter.1 = f32[2,8,1088,128]{3,2,1,0:T(8,128)} custom-call(f32[4]{0:T(128)} %pad_maximum_fusion.floats, f32[4,64,64,128]{3,2,1,0:T(8,128)} %bitcast.6, f32[4,64,64,128]{3,2,1,0:T(8,128)} %bitcast.7, f32[4,64,64,128]{3,2,1,0:T(8,128)} %bitcast.8, f32[4,64,64,128]{3,2,1,0:T(8,128)} %bitcast.13, f32[64,64,128]{2,1,0:T(8,128)} %diff.1, ...), custom_call_target="tpu_custom_call" | custom-call | tf_op jit(solution)/shard_map/enter/pallas_call | solution.py:764
  24.2 94.0 %spread.1 = f32[2,8,4,34,8,128]{5,4,3,2,1,0:T(8,128)} custom-call(f32[4]{0:T(128)} %pad_maximum_fusion.floats, f32[2,34]{1,0:T(2,128)} %constant.64.clone.wave_z, f32[2,8,4,34,8,128]{5,4,3,2,1,0:T(8,128)} %bitcast.11, f32[3,128,128]{2,1,0:T(8,128)} %constant.69.clone.refs_1_, bf16[256,256]{1,0:T(8,128)(2,1)} %constant.70.clone.refs_2_, ...), custom_call_target="tpu_custom_call" | custom-call | tf_op jit(solution)/shard_map/spread/pallas_call | solution.py:851
  118.2 17.2 %leave.1 = f32[4,64,64,128]{3,2,1,0:T(8,128)} custom-call(f32[4]{0:T(128)} %pad_maximum_fusion.floats, f32[2,8,1088,128]{3,2,1,0:T(8,128)} %bitcast.12, f32[4,64,64,128]{3,2,1,0:T(8,128)} %bitcast.10, bf16[256,256]{1,0:T(8,128)(2,1)} %constant.87.clone.y_high, bf16[256,256]{1,0:T(8,128)(2,1)} %constant.88.clone.y_low, ...), custom_call_target="tpu_custom_call" | custom-call | tf_op jit(solution)/shard_map/leave/pallas_call | solution.py:764

commit v4 on v3

--- a/solution.py
+++ b/solution.py
@@ -138,6 +138,10 @@
 
 def table_times(high, low, value):
     value_high, value_low = split(value)
+    if high.shape[1] <= 128 and value.shape[0] % 16 == 0:
+        twice = jnp.concatenate((high, high), axis=1)
+        both = jnp.concatenate((value_high, value_low), axis=0)
+        return dot(twice, both) + dot(low, value_high)
     return dot(high, value_high) + dot(high, value_low) + dot(low, value_high)
 
 
@@ -355,6 +359,7 @@
     def _():
         buffer[:, block + 1 :] = halo[1]
 
+    is_last = (step == plan.steps - 1).astype(jnp.float32)
     nodes = plan.matrix.sum(axis=1)
     size_z = plan.size_z
 
@@ -371,8 +376,8 @@
         transport = (
             floats[0] * (upper - lower) + floats[1] * (y_up - y_down) + floats[2] * (z_up - z_down)
         )
-        operated = floats[3] * (diffusion_number * laplace - 0.5 * transport)
-        kept = floats[3] * center
+        operated = is_last * (diffusion_number * laplace - 0.5 * transport)
+        kept = is_last * center
         result = []
         for row in range(4):
             total = right[row, plane] + (float(nodes[row]) * operated - kept)
@@ -691,7 +696,7 @@
     stages = (modes_stage, spectrum_stage, pair_stage, sweep_stage)
     stages += (start_stage, return_stage, solution_stage)
 
-    delays = (0, 1, 2, 3, 4, 5, 6)
+    delays = (0, 1, 2, 4, 6, 7, 8)
 
     def iteration(time, carry):
         for delay in range(len(stages)):
@@ -721,9 +726,10 @@
     lax.fori_loop(0, each, finish, 0)
 
 
-def leave_kernel(plan, floats, found_in, kept, y_high, y_low, z_high, z_low, z_rest, out):
+def leave_kernel(plan, found_in, kept, y_high, y_low, z_high, z_low, z_rest, out):
     block, rows, size_y, size_z = plan.block, plan.rows, plan.size_y, plan.size_z
     most = z_high.shape[1]
+    is_last = (lax.axis_index("tm") == plan.steps - 1).astype(jnp.float32)
 
     def pair(index, carry):
         plane = 2 * index
@@ -743,7 +749,7 @@
         if most < 2 * rows:
             found = found + dot(z_rest[...], tripled(stacked[most:]))
         for offset in range(2):
-            add = floats[3] * kept[0, plane + offset]
+            add = is_last * kept[0, plane + offset]
             for node in range(4):
                 part = found[node * size_z : (node + 1) * size_z]
                 out[node, plane + offset] = part[:, offset * size_y : (offset + 1) * size_y] + add
@@ -785,15 +791,13 @@
 def shards(iterate, right_side, diffusivity, velocity):
     steps = lax.axis_size("tm")
     slabs = lax.axis_size("space")
-    step = lax.axis_index("tm")
     nodes, long, size_z, size_y = iterate.shape[1:]
     plan = Plan(slabs, steps, long * slabs, size_z, size_y)
     size_x, padded, each = plan.size_x, plan.padded, plan.each
     rows, block, blocks, sent_rows, own = plan.rows, plan.block, plan.blocks, plan.sent, plan.own_x
     iterate, right_side = iterate[0], right_side[0]
 
-    is_last = (step == steps - 1).astype(jnp.float32)
-    floats = jnp.concatenate((velocity, is_last[None]))
+    floats = velocity
     wave_z = jnp.asarray(plan.z_symbols())
 
     z_tables = split_constant(plan.z_forward())
@@ -888,7 +892,6 @@
         "leave",
         (blocks,),
         [
-            scalars,
             pl.BlockSpec((2, 1, rows * block, size_y), lambda at: (0, at, 0, 0)),
             pl.BlockSpec((1, block, size_z, size_y), lambda at: (3, at, 0, 0)),
         ]
@@ -896,7 +899,6 @@
         pl.BlockSpec((4, block, size_z, size_y), lambda at: (0, at, 0, 0)),
         shaped(4, long, size_z, size_y),
         [
-            floats,
             spectrum.reshape(2, blocks, rows * block, size_y),
             iterate,
         ]

time: 136 us -> 126 us (0.926)
  Pallas kernels: 134 us -> 126 us
    pallas_call x1, Pallas kernels: 94 us -> 85.5 us  [shards(): pl.pallas_call(functools.partial(spread, plan), name='spread', in_specs=[...]
where the time goes in v4:
time: 126 us
  Pallas kernels  126 us (100%)
    pallas_call x1, Pallas kernels, shards(): pl.pallas_call(functools.partial(spread, plan), name='spread', in_specs=[...  85.5 us
    pallas_call x2, Pallas kernels, called(): pl.pallas_call(kernel, name=name, grid=grid, in_specs=in_specs, out_specs...  40.1 us

profile of v4, /device:TPU:0, one launch (start us, length us, event | category | flops | bytes accessed | tf_op | source)
XLA Modules:
  0.0 125.6 jit_solution(4188198119494420586)
XLA Ops:
  0.0 22.9 %enter.1 = f32[2,8,1088,128]{3,2,1,0:T(8,128)} custom-call(f32[3]{0:T(128)} %floats.3, f32[4,64,64,128]{3,2,1,0:T(8,128)} %bitcast.5, f32[4,64,64,128]{3,2,1,0:T(8,128)} %bitcast.6, f32[4,64,64,128]{3,2,1,0:T(8,128)} %bitcast.7, f32[4,64,64,128]{3,2,1,0:T(8,128)} %bitcast.12, f32[64,64,128]{2,1,0:T(8,128)} %diff.1, f32[4,64,64,128]{3,2,1,0:T(8,128)} %bitcast.8, ...), custom_call_target="tpu_custom_call" | custom-call | tf_op jit(solution)/shard_map/enter/pallas_call | solution.py:770
  22.9 85.5 %spread.1 = f32[2,8,4,34,8,128]{5,4,3,2,1,0:T(8,128)} custom-call(f32[3]{0:T(128)} %floats.3, f32[2,34]{1,0:T(2,128)} %constant.56.clone.wave_z, f32[2,8,4,34,8,128]{5,4,3,2,1,0:T(8,128)} %bitcast.10, f32[3,128,128]{2,1,0:T(8,128)} %constant.61.clone.refs_1_, bf16[256,256]{1,0:T(8,128)(2,1)} %constant.62.clone.refs_2_, ...), custom_call_target="tpu_custom_call" | custom-call | tf_op jit(solution)/shard_map/spread/pallas_call | solution.py:855
  108.5 17.2 %leave.1 = f32[4,64,64,128]{3,2,1,0:T(8,128)} custom-call(f32[2,8,1088,128]{3,2,1,0:T(8,128)} %bitcast.11, f32[4,64,64,128]{3,2,1,0:T(8,128)} %bitcast.9, bf16[256,256]{1,0:T(8,128)(2,1)} %constant.79.clone.y_high, bf16[256,256]{1,0:T(8,128)(2,1)} %constant.80.clone.y_low, bf16[256,256]{1,0:T(8,128)(2,1)} %constant.81.clone.z_high, ...), custom_call_target="tpu_custom_call" | custom-call | tf_op jit(solution)/shard_map/leave/pallas_call | solution.py:770
